TPU v7x, 8 devices: a whole 2x2x1 slice. The times are simulated.
8 devices in a mesh: dp: 2 (over z, y), ep: 4 (over x, core).
Axes of the slice: x: 2, y: 2, z: 1, core: 2. Of those that a mesh axis runs over, the one named last changes fastest.
Arguments:
- x_in: bfloat16 [16384, 1536], P(('dp', 'ep'))
- dy_in: bfloat16 [16384, 1536], P(('dp', 'ep'))
- top_ids: int32 [16384, 6], P(('dp', 'ep'))
- w_router: bfloat16 [1536, 64], P(('dp', 'ep'))
- w_gate: bfloat16 [64, 1536, 512], P('ep', 'dp')
- w_up: bfloat16 [64, 1536, 512], P('ep', 'dp')
- w_down: bfloat16 [64, 512, 1536], P('ep', 'dp')
- s_gate: bfloat16 [1536, 1024], P(('dp', 'ep'))
- s_up: bfloat16 [1536, 1024], P(('dp', 'ep'))
- s_down: bfloat16 [1024, 1536], P(('dp', 'ep'))
Outputs:
- output 1: bfloat16 [16384, 1536], P(('dp', 'ep'))
- output 2: bfloat16 [16384, 1536], P(('dp', 'ep'))
- output 3: float32 [1536, 64], P(('dp', 'ep'))
- output 4: float32 [64, 1536, 512], P('ep', 'dp')
- output 5: float32 [64, 1536, 512], P('ep', 'dp')
- output 6: float32 [64, 512, 1536], P('ep', 'dp')
- output 7: float32 [1536, 1024], P(('dp', 'ep'))
- output 8: float32 [1536, 1024], P(('dp', 'ep'))
- output 9: float32 [1024, 1536], P(('dp', 'ep'))
All inputs are finite; a program needn't handle non-finite values.
Results may differ from a plain program's by a relative error of at most 0.00497808.
Values are sent between devices in bfloat16 or wider.
A program may use at most 1 GiB of HBM per device.

v0:
```python
import jax
import jax.numpy as jnp
from jax import lax
from jax.sharding import PartitionSpec as P


def slot_tables(top_blk, num_experts, slot_cap):
    flat_ids = top_blk.reshape(-1)
    sort_order = jnp.argsort(flat_ids, stable=True)
    counts = jnp.bincount(flat_ids, length=num_experts)
    starts = jnp.cumsum(counts) - counts
    slot_idx = jnp.arange(slot_cap)
    is_valid = slot_idx[None, :] < counts[:, None]
    assign = sort_order[jnp.minimum(starts[:, None] + slot_idx[None, :], flat_ids.shape[0] - 1)]
    inverse = jnp.argsort(sort_order, stable=True)
    slot_pos = flat_ids * slot_cap + inverse - starts[flat_ids]
    return assign, is_valid, slot_pos


def silu_grads(d_hidden, gate_pre, up_pre):
    sig_gate = jax.nn.sigmoid(gate_pre)
    silu_gate = gate_pre * sig_gate
    d_gate = (d_hidden * up_pre * sig_gate * (1.0 + gate_pre * (1.0 - sig_gate))).astype(jnp.bfloat16)
    d_up = (d_hidden * silu_gate).astype(jnp.bfloat16)
    return d_gate, d_up


def solution(mesh):
    all_axes = ('dp', 'ep')
    ep_size = mesh.shape['ep']
    row_spec = P(all_axes, None)
    expert_spec = P('ep', 'dp', None)

    def local_step(x_loc, dy_loc, top_loc, wr_loc, wg_loc, wu_loc, wd_loc, sg_loc, su_loc, sd_loc):
        tok_count, top_k = top_loc.shape
        model_dim = x_loc.shape[1]
        num_experts = wr_loc.shape[1]
        local_experts = num_experts // ep_size
        slot_cap = 2 * tok_count * top_k // num_experts
        w_router = lax.all_gather(wr_loc, all_axes, axis=0, tiled=True)
        s_gate = lax.all_gather(sg_loc, all_axes, axis=0, tiled=True)
        s_up = lax.all_gather(su_loc, all_axes, axis=0, tiled=True)
        s_down = lax.all_gather(sd_loc, all_axes, axis=0, tiled=True)
        w_gate = lax.all_gather(wg_loc, 'dp', axis=1, tiled=True)
        w_up = lax.all_gather(wu_loc, 'dp', axis=1, tiled=True)
        w_down = lax.all_gather(wd_loc, 'dp', axis=1, tiled=True)

        logits = jnp.dot(x_loc, w_router, preferred_element_type=jnp.float32)
        router_prob = jax.nn.softmax(logits, axis=-1)
        gate_vals = jnp.take_along_axis(router_prob, top_loc, axis=1)
        assign, is_valid, slot_pos = slot_tables(top_loc, num_experts, slot_cap)
        src_tok = assign // top_k
        send_x = jnp.where(is_valid[:, :, None], x_loc[src_tok], 0)
        recv_x = lax.all_to_all(send_x, 'ep', 0, 0, tiled=True).reshape(ep_size, local_experts, slot_cap, model_dim)
        gate_pre = jnp.einsum('secd,edf->secf', recv_x, w_gate, preferred_element_type=jnp.float32)
        up_pre = jnp.einsum('secd,edf->secf', recv_x, w_up, preferred_element_type=jnp.float32)
        hidden = (jax.nn.silu(gate_pre) * up_pre).astype(jnp.bfloat16)
        out_rows = jnp.einsum('secf,efd->secd', hidden, w_down, preferred_element_type=jnp.float32).astype(jnp.bfloat16)
        back_rows = lax.all_to_all(out_rows.reshape(num_experts, slot_cap, model_dim), 'ep', 0, 0, tiled=True)
        out_tok = back_rows.reshape(num_experts * slot_cap, model_dim)[slot_pos].reshape(tok_count, top_k, model_dim)
        routed = jnp.sum(gate_vals[:, :, None] * out_tok, axis=1)
        sg_pre = jnp.dot(x_loc, s_gate, preferred_element_type=jnp.float32)
        su_pre = jnp.dot(x_loc, s_up, preferred_element_type=jnp.float32)
        s_hidden = (jax.nn.silu(sg_pre) * su_pre).astype(jnp.bfloat16)
        s_out = jnp.dot(s_hidden, s_down, preferred_element_type=jnp.float32)
        y_loc = (routed + s_out).astype(jnp.bfloat16)

        gate_grad = jnp.einsum('td,tkd->tk', dy_loc, out_tok, preferred_element_type=jnp.float32)
        slot_gate = jnp.where(is_valid, gate_vals.reshape(-1)[assign], 0.0)
        send_g = (slot_gate[:, :, None] * dy_loc[src_tok]).astype(jnp.bfloat16)
        recv_g = lax.all_to_all(send_g, 'ep', 0, 0, tiled=True).reshape(ep_size, local_experts, slot_cap, model_dim)
        d_hidden = jnp.einsum('secd,efd->secf', recv_g, w_down, preferred_element_type=jnp.float32)
        d_gate, d_up = silu_grads(d_hidden, gate_pre, up_pre)
        gw_down = jnp.einsum('secf,secd->efd', hidden, recv_g, preferred_element_type=jnp.float32)
        gw_gate = jnp.einsum('secd,secf->edf', recv_x, d_gate, preferred_element_type=jnp.float32)
        gw_up = jnp.einsum('secd,secf->edf', recv_x, d_up, preferred_element_type=jnp.float32)
        dx_rows = (jnp.einsum('secf,edf->secd', d_gate, w_gate, preferred_element_type=jnp.float32) + jnp.einsum('secf,edf->secd', d_up, w_up, preferred_element_type=jnp.float32)).astype(jnp.bfloat16)
        back_dx = lax.all_to_all(dx_rows.reshape(num_experts, slot_cap, model_dim), 'ep', 0, 0, tiled=True)
        dx_routed = jnp.sum(back_dx.reshape(num_experts * slot_cap, model_dim)[slot_pos].reshape(tok_count, top_k, model_dim), axis=1, dtype=jnp.float32)
        picked = top_loc[:, :, None] == jnp.arange(num_experts)[None, None, :]
        d_prob = jnp.sum(jnp.where(picked, gate_grad[:, :, None], 0.0), axis=1)
        d_logit = (router_prob * (d_prob - jnp.sum(router_prob * d_prob, axis=-1, keepdims=True))).astype(jnp.bfloat16)
        gw_router = jnp.einsum('td,te->de', x_loc, d_logit, preferred_element_type=jnp.float32)
        dx_router = jnp.einsum('te,de->td', d_logit, w_router, preferred_element_type=jnp.float32)
        ds_hidden = jnp.einsum('td,fd->tf', dy_loc, s_down, preferred_element_type=jnp.float32)
        ds_gate_pre, ds_up_pre = silu_grads(ds_hidden, sg_pre, su_pre)
        gs_down = jnp.einsum('tf,td->fd', s_hidden, dy_loc, preferred_element_type=jnp.float32)
        gs_gate = jnp.einsum('td,tf->df', x_loc, ds_gate_pre, preferred_element_type=jnp.float32)
        gs_up = jnp.einsum('td,tf->df', x_loc, ds_up_pre, preferred_element_type=jnp.float32)
        dx_shared = jnp.einsum('tf,df->td', ds_gate_pre, s_gate, preferred_element_type=jnp.float32) + jnp.einsum('tf,df->td', ds_up_pre, s_up, preferred_element_type=jnp.float32)
        dx_loc = (dx_routed + dx_shared + dx_router).astype(jnp.bfloat16)
        return (y_loc, dx_loc,
                lax.psum_scatter(gw_router, all_axes, scatter_dimension=0, tiled=True),
                lax.psum_scatter(gw_gate, 'dp', scatter_dimension=1, tiled=True),
                lax.psum_scatter(gw_up, 'dp', scatter_dimension=1, tiled=True),
                lax.psum_scatter(gw_down, 'dp', scatter_dimension=1, tiled=True),
                lax.psum_scatter(gs_gate, all_axes, scatter_dimension=0, tiled=True),
                lax.psum_scatter(gs_up, all_axes, scatter_dimension=0, tiled=True),
                lax.psum_scatter(gs_down, all_axes, scatter_dimension=0, tiled=True))

    return jax.shard_map(local_step, mesh=mesh,
                         in_specs=(row_spec, row_spec, row_spec, row_spec, expert_spec, expert_spec, expert_spec, row_spec, row_spec, row_spec),
                         out_specs=(row_spec, row_spec, row_spec, expert_spec, expert_spec, expert_spec, row_spec, row_spec, row_spec),
                         check_vma=False)
```

profile of v0, /device:TPU:0, one launch (start us, length us, event | category | flops | bytes accessed | tf_op | source)
XLA Modules:
  0.0 5957.1 jit_solution(9342690367216263556)
XLA Ops:
  8.0 1.2 copy.97
  10.8 85.2 %scatter_custom_fusion = s32[64]{0:T(128)S(1)} fusion(s32[12288]{0:T(1024)S(1)} %bitcast.208, s32[12288]{0:T(1024)S(1)} %broadcast.348, s32[]{:T(128)} %constant.16.clone.1), kind=kCustom, calls=%fused_computation.152 | custom fusion | flops 12288 | bytes 260 | tf_op jit(solution)/shard_map/scatter-add | solution.py:10
  97.7 8.2 sort.31
  105.9 135.5 %gather_fusion = s32[24576]{0:T(1024)S(1)} fusion(s32[12288]{0:T(1024)S(1)} %get-tuple-element.11, s32[24576]{0:T(1024)S(1)} %broadcast_clamp_fusion.2), kind=kCustom, calls=%fused_computation | custom fusion | bytes 294912 | tf_op jit(solution)/shard_map/gather | solution.py:14
  242.3 149.1 %gather_fusion.1 = bf16[24576,1536]{1,0:T(8,128)(2,1)} fusion(bf16[2048,1536]{1,0:T(8,128)(2,1)} %param.10, s32[24576]{0:T(1024)S(1)} %broadcast_clamp_fusion), kind=kCustom, calls=%fused_computation.1 | custom fusion | bytes 151093248 | tf_op jit(solution)/shard_map/gather | solution.py:53
  391.4 49.8 broadcast_select_fusion
  441.2 14.8 all-to-all-start
  458.2 296.2 %all-gather.8.cloned.1.call-done = bf16[16,1536,512]{2,1,0:T(8,128)(2,1)} async-done(((bf16[16,768,512]{2,1,0:T(8,128)(2,1)}), bf16[16,1536,512]{2,1,0:T(8,128)(2,1)}) %all-gather.8.cloned.1.call-update) | async-done | bytes 25165840 | tf_op jit(solution)/shard_map/all_gather | solution.py:44
  754.3 514.4 %all-to-all-done = bf16[64,384,1536]{2,1,0:T(8,128)(2,1)} async-done(((bf16[64,384,1536]{2,1,0:T(8,128)(2,1)}), bf16[64,384,1536]{2,1,0:T(8,128)(2,1)}, u32[]{:S(2)}, u32[]{:S(2)}) %all-to-all-start) | async-done | bytes 75497504 | tf_op jit(solution)/shard_map/all_to_all | solution.py:54
  1268.7 63.4 %fusion.8 = f32[16,4,384,512]{3,2,1,0:T(8,128)} fusion(bf16[4,16,384,1536]{3,2,1,0:T(8,128)(2,1)} %bitcast.5, bf16[16,1536,512]{2,1,0:T(8,128)(2,1)} %all-gather.8.cloned.1.call-done), kind=kOutput, calls=%fused_computation.21 | convolution fusion | flops 38654705664 | bytes 150994944 | tf_op jit(solution)/shard_map/secd,edf->secf/dot_general | solution.py:55
  1332.1 76.7 %fusion.14 = (bf16[4,16,384,512]{3,2,0,1:T(8,128)(2,1)}, f32[16,4,384,512]{3,2,1,0:T(8,128)}) fusion(f32[16,4,384,512]{3,2,1,0:T(8,128)} %fusion.8, bf16[16,1536,512]{2,1,0:T(8,128)(2,1)} %all-gather.10.cloned.1.call-done, bf16[4,16,384,1536]{3,2,1,0:T(8,128)(2,1)} %bitcast.5), kind=kOutput, calls=%fused_computation.30 | convolution fusion | flops 38730203136 | bytes 226492416 | tf_op jit(solution)/shard_map/secd,edf->secf/dot_general | solution.py:56
  1408.8 61.8 %convert_bitcast_fusion = bf16[4,16,384,1536]{3,2,0,1:T(8,128)(2,1)} fusion(bf16[4,16,384,512]{3,2,0,1:T(8,128)(2,1)} %get-tuple-element.190, bf16[16,512,1536]{2,1,0:T(8,128)(2,1)} %all-gather.12.cloned.1.call-done), kind=kOutput, calls=%fused_computation.13 | convolution fusion | flops 38692454400 | bytes 125829120 | tf_op jit(solution)/shard_map/secf,efd->secd/dot_general | solution.py:58
  1470.6 50.2 copy.102
  1520.8 14.9 all-to-all-start.1
  1535.8 8.2 sort.32
  1544.0 810.7 %all-gather = bf16[8,192,64]{1,2,0:T(8,128)(2,1)S(1)} all-gather(bf16[1,192,64]{1,2,0:T(8,128)(2,1)S(1)} %bitcast.209), channel_id=1, replica_groups=mesh['dp'=2,'ep'=4] {'dp','ep'}, dimensions={0}, use_global_device_ids=true | all-gather | bytes 221184 | tf_op jit(solution)/shard_map/all_gather | solution.py:40
  2354.8 0.9 reshape.560
  2356.1 1.3 reshape.399
  2357.5 149.6 %gather_fusion.4 = bf16[24576,1536]{1,0:T(8,128)(2,1)} fusion(bf16[2048,1536]{1,0:T(8,128)(2,1)} %param.11, s32[24576]{0:T(1024)S(1)} %copy-done.21), kind=kCustom, calls=%fused_computation.4 | custom fusion | bytes 151093248 | tf_op jit(solution)/shard_map/gather | solution.py:70
  2509.9 4.8 fusion.45
  2516.2 4.6 compare_select_fusion.4
  2520.8 10.3 compare_reduce_fusion.56
  2531.1 35.9 fusion.37
  2567.7 262.4 %gather_fusion.2 = bf16[12288,1536]{1,0:T(8,128)(2,1)} fusion(bf16[24576,1536]{1,0:T(8,128)(2,1)} %bitcast.16, s32[12288]{0:T(1024)S(1)} %fusion.37), kind=kCustom, calls=%fused_computation.2 | custom fusion | bytes 75546624 | tf_op jit(solution)/shard_map/gather | solution.py:60
  2830.1 56.9 reshape.275
  2887.0 39.4 fusion.31
  2928.3 98.0 %gather_fusion.6 = f32[12288]{0:T(1024)S(1)} fusion(f32[2048,64]{0,1:T(8,128)S(1)} %get-tuple-element.116, s32[12288]{0:T(1024)S(1)} %copy-done.4), kind=kCustom, calls=%fused_computation.6 | custom fusion | bytes 196608 | tf_op jit(solution)/shard_map/jit(take_along_axis)/gather | solution.py:50
  3026.4 1.0 reshape.402
  3028.8 135.5 %gather_fusion.3 = f32[24576]{0:T(1024)S(1)} fusion(f32[12288]{0:T(1024)S(1)} %select_n.96, s32[24576]{0:T(1024)S(1)} %copy-done.29), kind=kCustom, calls=%fused_computation.3 | custom fusion | bytes 294912 | tf_op jit(solution)/shard_map/gather | solution.py:69
  3164.5 50.3 fusion
  3214.8 14.6 all-to-all-start.2
  3231.3 41.4 all-gather.14.cloned.1.call-done
  3272.7 11.9 fusion.46
  3284.6 29.2 all-gather.16.cloned.1.call-done
  3313.8 11.7 fusion.47
  3325.5 29.4 all-gather.18.cloned.1.call-done
  3354.9 19.0 multiply_convert_fusion
  3374.7 4.0 convolution_bitcast_fusion.4
  3378.7 1.2 copy.123
  3380.0 12.3 convolution_bitcast_fusion.3
  3392.2 6.7 copy.125
  3399.0 11.9 convolution_bitcast_fusion.2
  3410.8 6.6 copy.127
  3417.5 11.9 fusion.50
  3429.5 728.8 %all-to-all-done.2 = bf16[64,384,1536]{2,1,0:T(8,128)(2,1)} async-done(((bf16[64,384,1536]{2,1,0:T(8,128)(2,1)}), bf16[64,384,1536]{2,1,0:T(8,128)(2,1)}, u32[]{:S(2)}, u32[]{:S(2)}) %all-to-all-start.2) | async-done | bytes 75497504 | tf_op jit(solution)/shard_map/all_to_all | solution.py:71
  4158.3 88.7 %fusion.13 = (bf16[4,16,384,512]{3,2,0,1:T(8,128)(2,1)}, bf16[4,16,384,512]{3,2,0,1:T(8,128)(2,1)}) fusion(f32[16,4,384,512]{3,2,1,0:T(8,128)} %fusion.8, f32[16,4,384,512]{3,2,1,0:T(8,128)} %get-tuple-element.191, bf16[16,512,1536]{2,1,0:T(8,128)(2,1)} %all-gather.12.cloned.1.call-done, bf16[4,16,384,1536]{3,2,1,0:T(8,128)(2,1)} %bitcast.83), kind=kOutput, calls=%fused_computation.28 | convolution fusion | flops 38818283520 | bytes 251658240 | tf_op jit(solution)/shard_map/secd,efd->secf/dot_general | solution.py:72
  4247.0 58.7 convolution_bitcast_fusion.1
  4305.7 58.8 convolution_bitcast_fusion
  4364.6 59.7 %fusion.19 = f32[16,512,1536]{2,1,0:T(8,128)} fusion(bf16[4,16,384,512]{3,2,0,1:T(8,128)(2,1)} %get-tuple-element.190, bf16[4,16,384,1536]{3,2,1,0:T(8,128)(2,1)} %bitcast.83), kind=kOutput, calls=%fused_computation.38 | convolution fusion | flops 38654705664 | bytes 150994944 | tf_op jit(solution)/shard_map/secf,secd->efd/dot_general | solution.py:74
  4424.3 70.7 %fusion.24 = f32[16,4,384,1536]{3,2,1,0:T(8,128)} fusion(bf16[4,16,384,512]{3,2,0,1:T(8,128)(2,1)} %get-tuple-element.120, bf16[16,1536,512]{2,1,0:T(8,128)(2,1)} %all-gather.8.cloned.1.call-done), kind=kOutput, calls=%fused_computation.43 | convolution fusion | flops 38654705664 | bytes 201326592 | tf_op jit(solution)/shard_map/secf,edf->secd/dot_general | solution.py:77
  4495.0 98.1 %fusion.1 = bf16[4,16,384,1536]{3,2,0,1:T(8,128)(2,1)} fusion(f32[16,4,384,1536]{3,2,1,0:T(8,128)} %fusion.24, bf16[4,16,384,512]{3,2,0,1:T(8,128)(2,1)} %get-tuple-element.119, bf16[16,1536,512]{2,1,0:T(8,128)(2,1)} %all-gather.10.cloned.1.call-done), kind=kOutput, calls=%fused_computation.12 | convolution fusion | flops 38730203136 | bytes 276824064 | tf_op jit(solution)/shard_map/secf,edf->secd/dot_general | solution.py:77
  4593.1 50.2 copy.105
  4643.3 14.9 all-to-all-start.3
  4658.2 11.7 fusion.48
  4669.9 9.3 fusion.49
  4679.2 131.6 %multiply_reduce_fusion = f32[2048,1536]{1,0:T(8,128)} fusion(bf16[2048,6,1536]{2,1,0:T(8,128)(2,1)} %reshape.275, f32[2048,6]{1,0:T(8,128)S(1)} %copy-done.6), kind=kLoop, calls=%fused_computation.11 | loop fusion | flops 53477376 | bytes 50380800 | tf_op jit(solution)/shard_map/reduce_sum | solution.py:61
  4810.9 13.2 add_convert_fusion.2
  4824.1 1.6 copy.124
  4825.7 644.4 %all-to-all-done.3 = bf16[64,384,1536]{2,1,0:T(8,128)(2,1)} async-done(((bf16[64,384,1536]{2,1,0:T(8,128)(2,1)}), bf16[64,384,1536]{2,1,0:T(8,128)(2,1)}, u32[]{:S(2)}, u32[]{:S(2)}) %all-to-all-start.3) | async-done | bytes 75497504 | tf_op jit(solution)/shard_map/all_to_all | solution.py:78
  5470.1 262.2 %gather_fusion.5 = bf16[12288,1536]{1,0:T(8,128)(2,1)} fusion(bf16[24576,1536]{1,0:T(8,128)(2,1)} %bitcast.90, s32[12288]{0:T(1024)S(1)} %copy-done.23), kind=kCustom, calls=%fused_computation.5 | custom fusion | bytes 75546624 | tf_op jit(solution)/shard_map/gather | solution.py:79
  5732.3 62.1 %reshape.279 = f32[2048,6,1536]{2,1,0:T(8,128)} reshape(bf16[12288,1536]{1,0:T(8,128)(2,1)} %gather_fusion.5) | data formatting | bytes 113246208 | tf_op jit(solution)/shard_map/convert_element_type | solution.py:79
  5794.4 43.5 reduce_sum.47
  5837.9 15.6 add_convert_fusion.1
  5853.6 96.1 %reduce-scatter.18.cloned.1.call-done = f32[16,256,1536]{2,1,0:T(8,128)} async-done(((f32[16,512,1536]{2,1,0:T(8,128)}), f32[16,256,1536]{2,1,0:T(8,128)}) %reduce-scatter.18.cloned.1.call-update) | async-done | bytes 25165840 | tf_op jit(solution)/shard_map/reduce_scatter | solution.py:96
  (157 shorter events, 18.0 us)
Async XLA Ops:
  9.9 231.5 %copy-start.24 = (s32[12288]{0:T(1024)}, s32[12288]{0:T(1024)S(1)}, u32[]{:S(2)}) copy-start(s32[12288]{0:T(1024)S(1)} %reshape.269) | copy-start | bytes 147460
  10.7 230.7 %copy-start.26 = (s32[12288,1]{0,1:T(1,128)}, s32[12288,1]{0,1:T(1,128)S(1)}, u32[]{:S(2)}) copy-start(s32[12288,1]{0,1:T(1,128)S(1)} %reshape.268) | copy-start | bytes 147460
  96.0 1.0 copy-start.37
  97.1 0.5 copy-start.13
  105.9 135.6 %copy-start.2 = (s32[12288]{0:T(1024)}, s32[12288]{0:T(1024)S(1)}, u32[]{:S(2)}) copy-start(s32[12288]{0:T(1024)S(1)} %get-tuple-element.11) | copy-start | bytes 147460
  242.3 149.1 %copy-start.20 = (s32[24576]{0:T(1024)}, s32[24576]{0:T(1024)S(1)}, u32[]{:S(2)}) copy-start(s32[24576]{0:T(1024)S(1)} %broadcast_clamp_fusion) | copy-start | bytes 294916
  242.3 149.1 %copy-start.30 = (pred[64,384]{1,0:T(8,128)(4,1)S(1)}, pred[64,384]{1,0:T(8,128)(4,1)}, u32[]{:S(2)}) copy-start(pred[64,384]{1,0:T(8,128)(4,1)} %iota_compare_fusion.1) | copy-start | bytes 73732
  441.2 827.6 %all-to-all-start = ((bf16[64,384,1536]{2,1,0:T(8,128)(2,1)}), bf16[64,384,1536]{2,1,0:T(8,128)(2,1)}, u32[]{:S(2)}, u32[]{:S(2)}) async-start(bf16[64,384,1536]{2,1,0:T(8,128)(2,1)} %broadcast_select_fusion), calls=%async_computation | async-start | bytes 150994944 | tf_op jit(solution)/shard_map/all_to_all | solution.py:54
  455.9 298.4 %all-gather.8.cloned.1.call-start = ((), (), s32[]{:S(2)}) async-start(), calls=%async_computation.11 | async-start | bytes 37748736 | tf_op jit(solution)/shard_map/all_gather | solution.py:44
  456.7 875.4 %all-gather.10.cloned.1.call-start = ((), (), s32[]{:S(2)}) async-start(), calls=%async_computation.12 | async-start | bytes 37748736 | tf_op jit(solution)/shard_map/all_gather | solution.py:45
  457.4 951.3 %all-gather.12.cloned.1.call-start = ((), (), s32[]{:S(2)}) async-start(), calls=%async_computation.13 | async-start | bytes 37748736 | tf_op jit(solution)/shard_map/all_gather | solution.py:46
  1520.8 14.9 copy-start.3
  1520.8 23.2 copy-start.36
  1520.8 834.9 %copy-start.17 = (s32[2048,6]{0,1:T(8,128)S(1)}, s32[2048,6]{0,1:T(8,128)}, u32[]{:S(2)}) copy-start(s32[2048,6]{0,1:T(8,128)} %param.12) | copy-start | bytes 147460
  1520.8 836.6 %copy-start.21 = (s32[24576]{0:T(1024)S(1)}, s32[24576]{0:T(1024)}, u32[]{:S(2)}) copy-start(s32[24576]{0:T(1024)} %copy-done.20) | copy-start | bytes 294916
  1520.8 1046.9 %all-to-all-start.1 = ((bf16[64,384,1536]{2,1,0:T(8,128)(2,1)}), bf16[64,384,1536]{2,1,0:T(8,128)(2,1)}, u32[]{:S(2)}, u32[]{:S(2)}) async-start(bf16[64,384,1536]{2,1,0:T(8,128)(2,1)} %bitcast.15), calls=%async_computation.1 | async-start | bytes 150994944 | tf_op jit(solution)/shard_map/all_to_all | solution.py:59
  2357.4 149.6 %copy-start.28 = (s32[64,384,1]{1,0,2:T(8,128)S(1)}, s32[64,384,1]{1,0,2:T(8,128)}, u32[]{:S(2)}) copy-start(s32[64,384,1]{1,0,2:T(8,128)} %get-tuple-element.124) | copy-start | bytes 294916
  2357.4 149.6 %copy-start.14 = (s32[64]{0:T(128)S(1)}, s32[64]{0:T(128)}, u32[]{:S(2)}) copy-start(s32[64]{0:T(128)} %copy-done.13) | copy-start | bytes 772
  2357.4 152.5 %copy-start.15 = (bf16[1536,64]{0,1:T(8,128)(2,1)S(1)}, bf16[1536,64]{0,1:T(8,128)(2,1)}, u32[]{:S(2)}) copy-start(bf16[1536,64]{0,1:T(8,128)(2,1)} %reshape.560) | copy-start | bytes 589828
  2357.5 158.8 %copy-start.27 = (s32[12288,1]{0,1:T(1,128)S(1)}, s32[12288,1]{0,1:T(1,128)}, u32[]{:S(2)}) copy-start(s32[12288,1]{0,1:T(1,128)} %copy-done.26) | copy-start | bytes 147460
  2357.5 173.6 %copy-start.25 = (s32[12288]{0:T(1024)S(1)}, s32[12288]{0:T(1024)}, u32[]{:S(2)}) copy-start(s32[12288]{0:T(1024)} %copy-done.24) | copy-start | bytes 147460
  2357.5 173.6 %copy-start.33 = (s32[12288]{0:T(1024)S(1)}, s32[12288]{0:T(1024)}, u32[]{:S(2)}) copy-start(s32[12288]{0:T(1024)} %get-tuple-element.12) | copy-start | bytes 147460
  2514.7 0.8 copy-start.9
  2514.7 6.0 copy-start.31
  2567.0 263.0 %copy-start.22 = (s32[12288]{0:T(1024)}, s32[12288]{0:T(1024)S(1)}, u32[]{:S(2)}) copy-start(s32[12288]{0:T(1024)S(1)} %fusion.37) | copy-start | bytes 147460
  2887.0 40.0 copy-start.18
  2887.0 40.5 copy-start.10
  2887.0 40.5 copy-start.32
  2887.0 40.5 copy-start.34
  2887.0 41.3 copy-start.4
  2927.5 0.8 copy-start.7
  2928.3 98.1 %copy-start = (f32[2048,64]{0,1:T(8,128)}, f32[2048,64]{0,1:T(8,128)S(1)}, u32[]{:S(2)}) copy-start(f32[2048,64]{0,1:T(8,128)S(1)} %get-tuple-element.116) | copy-start | bytes 1572868
  2928.3 99.4 %copy-start.19 = (s32[2048,6]{0,1:T(8,128)S(1)}, s32[2048,6]{0,1:T(8,128)}, u32[]{:S(2)}) copy-start(s32[2048,6]{0,1:T(8,128)} %param.12) | copy-start | bytes 147460
  2928.3 100.6 %copy-start.29 = (s32[24576]{0:T(1024)S(1)}, s32[24576]{0:T(1024)}, u32[]{:S(2)}) copy-start(s32[24576]{0:T(1024)} %broadcast_clamp_fusion.1) | copy-start | bytes 294916
  3028.1 136.3 %copy-start.5 = (f32[2048,6]{1,0:T(8,128)}, f32[2048,6]{1,0:T(8,128)S(1)}, u32[]{:S(2)}) copy-start(f32[2048,6]{1,0:T(8,128)S(1)} %copy.96) | copy-start | bytes 147460
  3028.8 135.6 %copy-start.38 = (s32[64]{0:T(128)S(1)}, s32[64]{0:T(128)}, u32[]{:S(2)}) copy-start(s32[64]{0:T(128)} %copy-done.37) | copy-start | bytes 772
  3214.8 943.4 %all-to-all-start.2 = ((bf16[64,384,1536]{2,1,0:T(8,128)(2,1)}), bf16[64,384,1536]{2,1,0:T(8,128)(2,1)}, u32[]{:S(2)}, u32[]{:S(2)}) async-start(bf16[64,384,1536]{2,1,0:T(8,128)(2,1)} %fusion), calls=%async_computation.2 | async-start | bytes 150994944 | tf_op jit(solution)/shard_map/all_to_all | solution.py:71
  3229.5 43.2 all-gather.14.cloned.1.call-start
  3230.0 83.8 %all-gather.16.cloned.1.call-start = ((), (), s32[]{:S(2)}) async-start(), calls=%async_computation.15 | async-start | bytes 3538944 | tf_op jit(solution)/shard_map/all_gather | solution.py:42
  3230.6 124.3 %all-gather.18.cloned.1.call-start = ((), (), s32[]{:S(2)}) async-start(), calls=%async_computation.16 | async-start | bytes 3538944 | tf_op jit(solution)/shard_map/all_gather | solution.py:43
  3231.2 1592.9 %reduce-scatter.22.cloned.1.call-start = ((), (), s32[]{:S(2)}) async-start(), calls=%async_computation.21 | async-start | bytes 884736
  3325.5 48.4 copy-start.1
  3325.5 48.4 copy-start.8
  3325.5 48.4 copy-start.35
  3374.0 0.7 copy-start.11
  3379.9 2473.6 %reduce-scatter.24.cloned.1.call-start = ((), (), s32[]{:S(2)}) async-start(), calls=%async_computation.22 | async-start | bytes 7077888
  3398.9 2454.6 %reduce-scatter.26.cloned.1.call-start = ((), (), s32[]{:S(2)}) async-start(), calls=%async_computation.23 | async-start | bytes 7077888
  3417.5 2436.0 %reduce-scatter.20.cloned.1.call-start = ((), (), s32[]{:S(2)}) async-start(), calls=%async_computation.20 | async-start | bytes 7077888 | tf_op jit(solution)/shard_map/reduce_scatter | solution.py:99
  3429.4 2424.1 %reduce-scatter.14.cloned.1.call-start = ((), (), s32[]{:S(2)}) async-start(), calls=%async_computation.17 | async-start | bytes 75497472 | tf_op jit(solution)/shard_map/reduce_scatter | solution.py:94
  4305.7 1547.9 %reduce-scatter.16.cloned.1.call-start = ((), (), s32[]{:S(2)}) async-start(), calls=%async_computation.18 | async-start | bytes 75497472 | tf_op jit(solution)/shard_map/reduce_scatter | solution.py:95
  4364.5 1585.2 %reduce-scatter.18.cloned.1.call-start = ((), (), s32[]{:S(2)}) async-start(), calls=%async_computation.19 | async-start | bytes 75497472 | tf_op jit(solution)/shard_map/reduce_scatter | solution.py:96
  4643.3 14.9 copy-start.39
  4643.3 826.8 %all-to-all-start.3 = ((bf16[64,384,1536]{2,1,0:T(8,128)(2,1)}), bf16[64,384,1536]{2,1,0:T(8,128)(2,1)}, u32[]{:S(2)}, u32[]{:S(2)}) async-start(bf16[64,384,1536]{2,1,0:T(8,128)(2,1)} %bitcast.89), calls=%async_computation.3 | async-start | bytes 150994944 | tf_op jit(solution)/shard_map/all_to_all | solution.py:78
  4658.2 11.7 copy-start.40
  4658.2 11.7 copy-start.41
  4669.9 9.3 copy-start.6
  4810.9 659.2 %copy-start.23 = (s32[12288]{0:T(1024)S(1)}, s32[12288]{0:T(1024)}, u32[]{:S(2)}) copy-start(s32[12288]{0:T(1024)} %copy-done.22) | copy-start | bytes 147460
  5794.4 43.5 copy-start.12
  5794.4 43.5 copy-start.16
Sparse Core Ops, SparseCore 0:
  458.3 296.0 all-gather.7
  755.9 292.7 all-gather.9
  1050.1 292.7 all-gather.11
Sparse Core Ops, SparseCore 1:
  3231.8 40.9 all-gather.13
  3274.4 39.4 all-gather.15
  3315.5 39.4 all-gather.17
  3380.0 29.8 reduce-scatter.21
  3413.7 78.7 reduce-scatter.23
  3496.4 78.7 reduce-scatter.25
  3578.8 78.7 reduce-scatter.19
  4305.7 546.1 reduce-scatter.13
  4854.6 546.0 reduce-scatter.15
  5403.6 546.0 reduce-scatter.17
where the time goes:
time: 5980 us; the launch traced here: 5960 us
  waiting for transfers between devices  2380 us (40%)
  local copies, waits for them, and re-layouts  1440 us (24%)
  matrix products  813 us (14%)
  blocking collectives  811 us (14%)
  other arithmetic  432 us (7%)
    all_gather x1, blocking collectives, local_step(): w_router = lax.all_gather(wr_loc, all_axes, axis=0, tiled=True)  811 us
    all_to_all x1, waiting for transfers between devices, local_step(): lax.all_to_all(send_g, 'ep', 0, 0, tiled=True)  729 us
    all_to_all x1, waiting for transfers between devices, local_step(): lax.all_to_all(dx_rows.reshape(num_experts, slot_cap, model_dim), 'ep', 0...  644 us
    all_to_all x1, waiting for transfers between devices, local_step(): lax.all_to_all(send_x, 'ep', 0, 0, tiled=True)  514 us
    all_gather x1, waiting for transfers between devices, local_step(): w_gate = lax.all_gather(wg_loc, 'dp', axis=1, tiled=True)  296 us
    gather x1, local copies, waits for them, and re-layouts, local_step(): back_rows.reshape(num_experts * slot_cap, model_dim)[slot_pos]  262 us
    gather x1, local copies, waits for them, and re-layouts, local_step(): back_dx.reshape(num_experts * slot_cap, model_dim)[slot_pos]  262 us
    gather x1, local copies, waits for them, and re-layouts, local_step(): send_g = (slot_gate[:, :, None] * dy_loc[src_tok]).astype(jnp.bfloat16)  150 us
  transfers between devices with their start and end apart: 17, of which 8 were waited for; matrix products, arithmetic and copies ran while one was open for 25% of the time, Pallas kernels for 0%

commit v1 on v0

v1 whole, which is shorter than its diff:
```python
import functools
import jax
import jax.numpy as jnp
from jax import lax
from jax.experimental import pallas as pl
from jax.experimental.pallas import tpu as pltpu
from jax.sharding import PartitionSpec as P

F32 = jnp.float32
BF16 = jnp.bfloat16
CHUNKS = 4
GROUP = 8


def silu_grads(d_hidden, gate_pre, up_pre):
    sig_gate = jax.nn.sigmoid(gate_pre)
    silu_gate = gate_pre * sig_gate
    d_gate = (d_hidden * up_pre * sig_gate * (1.0 + gate_pre * (1.0 - sig_gate))).astype(BF16)
    d_up = (d_hidden * silu_gate).astype(BF16)
    return d_gate, d_up


def combine_kernel(num_parts, per_part, slot_cap, weighted, first_blk, cnt_ref, tok_ref, gate_ref, *refs):
    parts, out_ref, buf = refs[:num_parts], refs[num_parts], refs[num_parts + 1]
    blk, exp = pl.program_id(0), pl.program_id(1)
    group_id = (blk + first_blk) * (num_parts * per_part) + exp

    @pl.when(exp == 0)
    def _():
        out_ref[...] = jnp.zeros_like(out_ref)

    for part in range(num_parts):
        @pl.when(exp // per_part == part)
        def _(part=part):
            buf[...] = parts[part][0, 0].astype(F32)

    count = cnt_ref[group_id]
    base = group_id * slot_cap

    def add_rows(first, num):
        toks = [tok_ref[base + first + u] for u in range(num)]
        rows = []
        for u in range(num):
            row = buf[pl.ds(first + u, 1), :]
            if weighted:
                row = row * gate_ref[base + first + u]
            rows.append(out_ref[0, pl.ds(toks[u], 1), :] + row)
        for u in range(num):
            out_ref[0, pl.ds(toks[u], 1), :] = rows[u]

    def full_step(i, carry):
        add_rows(i * GROUP, GROUP)
        return carry

    def tail_step(i, carry):
        add_rows(i, 1)
        return carry

    full = count // GROUP
    lax.fori_loop(0, full, full_step, 0)
    lax.fori_loop(full * GROUP, count, tail_step, 0)


def combine(parts, counts, toks, gates, tok_count, weighted, first, blocks):
    num_parts = len(parts)
    per_part, _, slot_cap, dim = parts[0].shape

    def part_map(part, b, e, *_):
        return (jnp.clip(e - part * per_part, 0, per_part - 1), b + first, 0, 0)

    return pl.pallas_call(
        functools.partial(combine_kernel, num_parts, per_part, slot_cap, weighted, first),
        grid_spec=pltpu.PrefetchScalarGridSpec(
            num_scalar_prefetch=3,
            grid=(blocks, num_parts * per_part),
            in_specs=[pl.BlockSpec((1, 1, slot_cap, dim), functools.partial(part_map, part)) for part in range(num_parts)],
            out_specs=pl.BlockSpec((1, tok_count, dim), lambda b, e, *_: (b, 0, 0)),
            scratch_shapes=[pltpu.VMEM((slot_cap, dim), F32)],
        ),
        out_shape=jax.ShapeDtypeStruct((blocks, tok_count, dim), F32),
        compiler_params=pltpu.CompilerParams(
            dimension_semantics=("arbitrary", "arbitrary"), vmem_limit_bytes=56 * 1024 * 1024),
        cost_estimate=pl.CostEstimate(flops=20_000_000_000, bytes_accessed=130_000_000, transcendentals=0),
    )(counts, toks, gates, *parts)


def solution(mesh):
    all_axes = ('dp', 'ep')
    ep_size = mesh.shape['ep']
    row_spec = P(all_axes, None)
    expert_spec = P('ep', 'dp', None)
    swap_chip = [(i, i ^ 2) for i in range(ep_size)]
    swap_core = [(i, i ^ 1) for i in range(ep_size)]
    swap_both = [(i, i ^ 3) for i in range(ep_size)]
    swap_dp = [(0, 1), (1, 0)]

    def spread(val):
        chip_val = lax.ppermute(val, 'ep', swap_chip)
        core_val = lax.ppermute(val, 'ep', swap_core)
        both_val = lax.ppermute(chip_val, 'ep', swap_core)
        return lax.optimization_barrier(jnp.stack([val, chip_val, core_val, both_val]))

    def collect(near, far):
        recv = lax.ppermute(far, 'ep', swap_core)
        return near[0] + recv[0] + lax.ppermute(near[1] + recv[1], 'ep', swap_chip)

    def local_step(x_loc, dy_loc, top_loc, wr_loc, wg_loc, wu_loc, wd_loc, sg_loc, su_loc, sd_loc):
        tok_count, top_k = top_loc.shape
        num_experts = wr_loc.shape[1]
        local_experts = num_experts // ep_size
        per_chunk = local_experts // CHUNKS
        slot_cap = 2 * tok_count * top_k // num_experts
        dp_idx = lax.axis_index('dp')
        ep_idx = lax.axis_index('ep')

        def gather_dp(shard):
            recv = lax.ppermute(shard, 'dp', swap_dp)
            return jnp.where(dp_idx == 0, jnp.concatenate([shard, recv], axis=1), jnp.concatenate([recv, shard], axis=1))

        def split_dp(full):
            half = full.shape[1] // 2
            return lax.dynamic_slice_in_dim(full, (1 - dp_idx) * half, half, axis=1), lax.dynamic_slice_in_dim(full, dp_idx * half, half, axis=1)

        shards = [[w[ci * per_chunk:(ci + 1) * per_chunk] for w in (wd_loc, wg_loc, wu_loc)] for ci in range(CHUNKS)]
        shards, x_loc, dy_loc, top_loc, wr_loc = lax.optimization_barrier((shards, x_loc, dy_loc, top_loc, wr_loc))
        chunk_w = [[gather_dp(w) for w in shards[ci]] for ci in range(CHUNKS)]

        x_all = spread(x_loc)
        dy_all = spread(dy_loc)
        w_router = lax.all_gather(wr_loc, all_axes, axis=0, tiled=True)
        s_gate = lax.all_gather(sg_loc, all_axes, axis=0, tiled=True)
        s_up = lax.all_gather(su_loc, all_axes, axis=0, tiled=True)
        s_down = lax.all_gather(sd_loc, all_axes, axis=0, tiled=True)

        logits = jnp.dot(x_loc, w_router, preferred_element_type=F32)
        router_prob = jax.nn.softmax(logits, axis=-1)
        picked = jnp.any(top_loc[:, :, None] == jnp.arange(num_experts)[None, None, :], axis=1)
        tok_ids = jnp.arange(tok_count)
        before = (tok_ids[None, :] < tok_ids[:, None]).astype(BF16)
        rank = jnp.dot(before, picked.astype(BF16), preferred_element_type=F32)
        slot_of = jnp.where(picked, rank, -1.0).T
        slot_ids = jnp.arange(slot_cap, dtype=F32)
        at_slot = slot_of[:, None, :] == slot_ids[None, :, None]
        tok_tab = jnp.sum(jnp.where(at_slot, (tok_ids + 1).astype(F32)[None, None, :], 0.0), axis=-1) - 1.0
        gate_tab = jnp.sum(jnp.where(at_slot, router_prob.T[:, None, :], 0.0), axis=-1)
        tabs = spread(jnp.stack([tok_tab, gate_tab]))
        tabs = lax.dynamic_slice_in_dim(tabs, ep_idx * local_experts, local_experts, axis=2)
        toks = tabs[:, 0].astype(jnp.int32)
        gates = tabs[:, 1]

        sg_pre = jnp.dot(x_loc, s_gate, preferred_element_type=F32)
        su_pre = jnp.dot(x_loc, s_up, preferred_element_type=F32)
        s_hidden = (jax.nn.silu(sg_pre) * su_pre).astype(BF16)
        s_out = jnp.dot(s_hidden, s_down, preferred_element_type=F32)
        ds_hidden = jnp.einsum('td,fd->tf', dy_loc, s_down, preferred_element_type=F32)
        ds_gate_pre, ds_up_pre = silu_grads(ds_hidden, sg_pre, su_pre)
        gs_down = jnp.einsum('tf,td->fd', s_hidden, dy_loc, preferred_element_type=F32)
        gs_gate = jnp.einsum('td,tf->df', x_loc, ds_gate_pre, preferred_element_type=F32)
        gs_up = jnp.einsum('td,tf->df', x_loc, ds_up_pre, preferred_element_type=F32)
        dx_shared = jnp.einsum('tf,df->td', ds_gate_pre, s_gate, preferred_element_type=F32) + jnp.einsum('tf,df->td', ds_up_pre, s_up, preferred_element_type=F32)

        toks, gs_gate, gs_up, gs_down, dx_shared, s_out = lax.optimization_barrier((toks, gs_gate, gs_up, gs_down, dx_shared, s_out))
        gs_gate, gs_up, gs_down = [lax.psum_scatter(g, all_axes, scatter_dimension=0, tiled=True) for g in (gs_gate, gs_up, gs_down)]
        out_parts, dx_parts, q_parts = [], [], []
        grads = []
        for ci in range(CHUNKS):
            w_down, w_gate, w_up = chunk_w[ci]
            sl = slice(ci * per_chunk, (ci + 1) * per_chunk)
            tok_c, gate_c = toks[:, sl], gates[:, sl]
            pick = (tok_c[..., None] == tok_ids).astype(BF16)
            rows_x = jnp.einsum('bect,btd->becd', pick, x_all, preferred_element_type=F32).astype(BF16)
            rows_dy = jnp.einsum('bect,btd->becd', pick, dy_all, preferred_element_type=F32).astype(BF16)
            rows_g = (gate_c[..., None] * rows_dy).astype(BF16)
            gate_pre = jnp.einsum('becd,edf->ebcf', rows_x, w_gate, preferred_element_type=F32)
            up_pre = jnp.einsum('becd,edf->ebcf', rows_x, w_up, preferred_element_type=F32)
            hidden = (jax.nn.silu(gate_pre) * up_pre).astype(BF16)
            out_rows = jnp.einsum('ebcf,efd->ebcd', hidden, w_down, preferred_element_type=F32).astype(BF16)
            q_parts.append(jnp.einsum('becd,ebcd->bec', rows_dy, out_rows, preferred_element_type=F32))
            d_hidden = jnp.einsum('becd,efd->ebcf', rows_g, w_down, preferred_element_type=F32)
            d_gate, d_up = silu_grads(d_hidden, gate_pre, up_pre)
            sent_down, kept_down = split_dp(jnp.einsum('ebcf,becd->efd', hidden, rows_g, preferred_element_type=F32))
            sent_gate, kept_gate = split_dp(jnp.einsum('becd,ebcf->edf', rows_x, d_gate, preferred_element_type=F32))
            sent_up, kept_up = split_dp(jnp.einsum('becd,ebcf->edf', rows_x, d_up, preferred_element_type=F32))
            dx_rows = (jnp.einsum('ebcf,edf->ebcd', d_gate, w_gate, preferred_element_type=F32) + jnp.einsum('ebcf,edf->ebcd', d_up, w_up, preferred_element_type=F32)).astype(BF16)
            toks, sent_down, sent_gate, sent_up, out_rows, dx_rows = lax.optimization_barrier((toks, sent_down, sent_gate, sent_up, out_rows, dx_rows))
            if ci == CHUNKS - 2:
                toks, gs_gate, gs_up, gs_down = lax.optimization_barrier((toks, gs_gate, gs_up, gs_down))
            recvs = [lax.ppermute(val, 'dp', swap_dp) for val in (sent_down, sent_gate, sent_up)]
            grads.append(([kept_down, kept_gate, kept_up], recvs))
            out_parts.append(out_rows)
            dx_parts.append(dx_rows)

        counts = jnp.sum((toks >= 0).astype(jnp.int32), axis=-1).reshape(-1)
        safe_toks = jnp.maximum(toks, 0).reshape(-1)
        flat_gates = gates.reshape(-1)
        near_cnt = ep_size // 2

        def join(parts, weighted):
            far = combine(parts, counts, safe_toks, flat_gates, tok_count, weighted, near_cnt, ep_size - near_cnt)
            near = combine(parts, counts, safe_toks, flat_gates, tok_count, weighted, 0, near_cnt)
            return collect(near, far)

        y_loc = (join(out_parts, True) + s_out).astype(BF16)
        dx_routed = join(dx_parts, False)

        q_tab = jnp.concatenate(q_parts, axis=1)
        q_from = [q_tab[0], lax.ppermute(q_tab[1], 'ep', swap_chip), lax.ppermute(q_tab[2], 'ep', swap_core), lax.ppermute(q_tab[3], 'ep', swap_both)]
        q_all = jnp.zeros((num_experts, slot_cap), F32)
        for rel, q_blk in zip((0, 2, 1, 3), q_from):
            q_all = lax.dynamic_update_slice_in_dim(q_all, q_blk, (ep_idx ^ rel) * local_experts, axis=0)
        d_prob = jnp.sum(jnp.where(at_slot, q_all[:, :, None], 0.0), axis=1).T
        d_logit = (router_prob * (d_prob - jnp.sum(router_prob * d_prob, axis=-1, keepdims=True))).astype(BF16)
        gw_router = jnp.einsum('td,te->de', x_loc, d_logit, preferred_element_type=F32)
        dx_router = jnp.einsum('te,de->td', d_logit, w_router, preferred_element_type=F32)
        dx_loc = (dx_routed + dx_shared + dx_router).astype(BF16)
        grads[-1][0][:], y_loc, dx_loc = lax.optimization_barrier((grads[-1][0], y_loc, dx_loc))
        totals = [jnp.zeros(w.shape, F32) for w in (wd_loc, wg_loc, wu_loc)]
        for ci, (kept, recvs) in enumerate(grads):
            totals = [lax.dynamic_update_slice(tot, k + r, (ci * per_chunk, 0, 0)) for tot, k, r in zip(totals, kept, recvs)]
        gw_down, gw_gate, gw_up = totals
        return (y_loc, dx_loc,
                lax.psum_scatter(gw_router, all_axes, scatter_dimension=0, tiled=True),
                gw_gate, gw_up, gw_down, gs_gate, gs_up, gs_down)

    return jax.shard_map(local_step, mesh=mesh,
                         in_specs=(row_spec, row_spec, row_spec, row_spec, expert_spec, expert_spec, expert_spec, row_spec, row_spec, row_spec),
                         out_specs=(row_spec, row_spec, row_spec, expert_spec, expert_spec, expert_spec, row_spec, row_spec, row_spec),
                         check_vma=False)
```

time: 5980 us -> 3820 us (0.64)
  local copies, waits for them, and re-layouts: 1440 us -> 167 us
  blocking collectives: 811 us -> 15.3 us
  waiting for transfers between devices: 2380 us -> 1610 us
  matrix products: 813 us -> 1380 us
  Pallas kernels: 0 us -> 254 us
  other arithmetic: 432 us -> 325 us
    all_to_all x4 -> x0, waiting for transfers between devices: 1890 us -> none  [the longest x1 729 us: local_step(): lax.all_to_all(send_g, 'ep', 0, 0, tiled=True)]
    ppermute x0 -> x40, waiting for transfers between devices: none -> 1580 us  [the longest x12 1210 us: local_step(): lax.ppermute(val, 'dp', swap_dp)]
    gather x17 -> x0, local copies, waits for them, and re-layouts: 1200 us -> none  [the longest x1 262 us: local_step(): back_rows.reshape(num_experts * slot_cap, model_dim)[slot_pos]]
    all_gather x1, blocking collectives: 811 us -> 15.3 us  [local_step(): w_router = lax.all_gather(wr_loc, all_axes, axis=0, tiled=True)]
    dot_general x22 -> x56, matrix products: 813 us -> 1370 us  [the longest x4 203 us: local_step(): jnp.einsum('bect,btd->becd', pick, dy_all, preferred_element_type=F32)]
    all_gather x3 -> x0, waiting for transfers between devices: 296 us -> none  [the longest x1 296 us: local_step(): w_gate = lax.all_gather(wg_loc, 'dp', axis=1, tiled=True)]
    pallas_call x0 -> x4, Pallas kernels: none -> 254 us  [combine(): pl.pallas_call(functools.partial(combine_kernel, num_parts, per_part, slo...]
    convert_element_type x3 -> x0, local copies, waits for them, and re-layouts: 162 us -> none  [the longest x1 62.1 us: local_step(): jnp.sum(back_dx.reshape(num_experts * slot_cap, model_dim)[slot_pos].resh...]
  transfers between devices with their start and end apart: 17 -> 47, of which waited for: 8 -> 20; matrix products, arithmetic and copies ran while one was open for 25% -> 41% of each run, Pallas kernels for 0% -> 5%
where the time goes in v1:
time: 3820 us; the launch traced here: 3810 us
  waiting for transfers between devices  1610 us (42%)
  matrix products  1380 us (36%)
  other arithmetic  325 us (9%)
  Pallas kernels  254 us (7%)
  local copies, waits for them, and re-layouts  167 us (4%)
  starting transfers between devices  49.9 us (1%)
    ppermute x12, waiting for transfers between devices, local_step(): lax.ppermute(val, 'dp', swap_dp)  1210 us
    ppermute x3, waiting for transfers between devices, spread(): chip_val = lax.ppermute(val, 'ep', swap_chip)  326 us
    pallas_call x4, Pallas kernels, combine(): pl.pallas_call(functools.partial(combine_kernel, num_parts, per_part, slo...  254 us
    dot_general x4, matrix products, local_step(): jnp.einsum('bect,btd->becd', pick, dy_all, preferred_element_type=F32)  203 us
    dot_general x4, matrix products, local_step(): jnp.einsum('bect,btd->becd', pick, x_all, preferred_element_type=F32)  198 us
    dot_general x4, matrix products, local_step(): jnp.einsum('becd,efd->ebcf', rows_g, w_down, preferred_element_type=F32)  114 us
    dot_general x4, matrix products, local_step(): jnp.einsum('ebcf,edf->ebcd', d_gate, w_gate, preferred_element_type=F32)  112 us
    reduce_sum x1, other arithmetic, local_step(): jnp.sum(jnp.where(at_slot, (tok_ids + 1).astype(F32)[None, None, :], 0.0)...  108 us
  transfers between devices with their start and end apart: 47, of which 20 were waited for; matrix products, arithmetic and copies ran while one was open for 41% of the time, Pallas kernels for 5%

profile of v1, /device:TPU:0, one launch (start us, length us, event | category | flops | bytes accessed | tf_op | source)
XLA Modules:
  0.0 3814.7 jit_solution(3057935872794343114)
XLA Ops:
  59.5 107.8 %select_reduce_fusion.2 = (f32[64,384]{1,0:T(8,128)S(1)}, f32[64,384]{1,0:T(8,128)S(1)}) fusion(f32[2048]{0:T(1024)S(1)} %add_convert_fusion.4, f32[64,2048]{1,0:T(8,128)S(1)} %fusion.154, f32[64,2048]{1,0:T(8,128)S(1)} %fusion.187), kind=kLoop, calls=%fused_computation.2 | loop fusion | flops 251609088 | bytes 1253376 | tf_op jit(solution)/shard_map/reduce_sum | solution.py:144
  290.6 187.1 %collective-permute-done.8 = bf16[2048,1536]{1,0:T(8,128)(2,1)} collective-permute-done((bf16[2048,1536]{1,0:T(8,128)(2,1)}, bf16[2048,1536]{1,0:T(8,128)(2,1)}, u32[]{:S(2)}, u32[]{:S(2)}) %collective-permute-start.8) | collective-permute-done | bytes 6291488 | tf_op jit(solution)/shard_map/ppermute | solution.py:98
  478.3 133.5 %collective-permute-done.3 = bf16[2048,1536]{1,0:T(8,128)(2,1)} collective-permute-done((bf16[2048,1536]{1,0:T(8,128)(2,1)}, bf16[2048,1536]{1,0:T(8,128)(2,1)}, u32[]{:S(2)}, u32[]{:S(2)}) %collective-permute-start.3) | collective-permute-done | bytes 6291488 | tf_op jit(solution)/shard_map/ppermute | solution.py:98
  615.9 22.5 pad_maximum_fusion.1
  658.8 50.6 %multiply_convert_fusion.3 = (bf16[4,4,384,1536]{3,2,1,0:T(8,128)(2,1)}, f32[4,4,384,1536]{3,2,1,0:T(8,128)}) fusion(f32[4,4,384]{2,1,0:T(4,128)S(1)} %get-tuple-element.166, bf16[4,2048,1536]{2,1,0:T(8,128)(2,1)} %pad_maximum_fusion.1, s32[4,4,384]{2,1,0:T(4,128)S(1)} %slice.115), kind=kOutput, calls=%fused_computation.27 | convolution fusion | flops 38705037312 | bytes 81838080 | tf_op jit(solution)/shard_map/bect,btd->becd/dot_general | solution.py:172
  709.4 49.5 %fusion.57 = bf16[4,4,384,1536]{3,2,1,0:T(8,128)(2,1)} fusion(bf16[4,2048,1536]{2,1,0:T(8,128)(2,1)} %pad_maximum_fusion, s32[4,4,384]{2,1,0:T(4,128)S(1)} %slice.115), kind=kOutput, calls=%fused_computation.84 | convolution fusion | flops 38676725760 | bytes 44064768 | tf_op jit(solution)/shard_map/bect,btd->becd/dot_general | solution.py:171
  776.4 21.2 fusion.53
  799.0 23.0 fusion.55
  822.0 21.2 collective-permute-done.11
  843.8 28.0 multiply_convert_fusion.13
  871.8 20.2 fusion.93
  892.0 18.4 convolution_bitcast_fusion.6
  910.4 18.4 convolution_bitcast_fusion.7
  947.4 22.0 fusion.148
  969.3 27.1 multiply_reduce_fusion.3
  996.5 28.0 add_convert_fusion.3.refs_0_
  1025.3 51.0 %multiply_convert_fusion.2 = (bf16[4,4,384,1536]{3,2,1,0:T(8,128)(2,1)}, f32[4,4,384,1536]{3,2,1,0:T(8,128)}) fusion(f32[4,4,384]{2,1,0:T(4,128)S(1)} %copy-done.24, bf16[4,2048,1536]{2,1,0:T(8,128)(2,1)} %pad_maximum_fusion.1, s32[4,4,384]{2,1,0:T(4,128)S(1)} %slice.118), kind=kOutput, calls=%fused_computation.25 | convolution fusion | flops 38705037312 | bytes 81838080 | tf_op jit(solution)/shard_map/bect,btd->becd/dot_general | solution.py:172
  1076.3 49.4 %fusion.62 = bf16[4,4,384,1536]{3,2,1,0:T(8,128)(2,1)} fusion(bf16[4,2048,1536]{2,1,0:T(8,128)(2,1)} %pad_maximum_fusion, s32[4,4,384]{2,1,0:T(4,128)S(1)} %slice.118), kind=kOutput, calls=%fused_computation.85 | convolution fusion | flops 38676725760 | bytes 44064768 | tf_op jit(solution)/shard_map/bect,btd->becd/dot_general | solution.py:171
  1127.0 23.2 fusion.45
  1150.9 22.9 fusion.47
  1175.2 28.6 multiply_convert_fusion.10
  1203.8 20.1 fusion.96
  1229.8 18.6 convolution_bitcast_fusion.4
  1278.6 21.9 fusion.141
  1300.6 26.6 multiply_reduce_fusion.2
  1327.2 28.3 add_convert_fusion.2.refs_1_
  1356.3 50.9 %multiply_convert_fusion.1 = (bf16[4,4,384,1536]{3,2,1,0:T(8,128)(2,1)}, f32[4,4,384,1536]{3,2,1,0:T(8,128)}) fusion(f32[4,4,384]{2,1,0:T(4,128)S(1)} %copy-done.23, bf16[4,2048,1536]{2,1,0:T(8,128)(2,1)} %pad_maximum_fusion.1, s32[4,4,384]{2,1,0:T(4,128)S(1)} %slice.120), kind=kOutput, calls=%fused_computation.23 | convolution fusion | flops 38705037312 | bytes 81838080 | tf_op jit(solution)/shard_map/bect,btd->becd/dot_general | solution.py:172
  1407.1 49.4 %fusion.67 = bf16[4,4,384,1536]{3,2,1,0:T(8,128)(2,1)} fusion(bf16[4,2048,1536]{2,1,0:T(8,128)(2,1)} %pad_maximum_fusion, s32[4,4,384]{2,1,0:T(4,128)S(1)} %slice.120), kind=kOutput, calls=%fused_computation.86 | convolution fusion | flops 38676725760 | bytes 44064768 | tf_op jit(solution)/shard_map/bect,btd->becd/dot_general | solution.py:171
  1457.2 23.5 fusion.37
  1480.7 23.2 fusion.39
  1503.9 28.9 multiply_convert_fusion.7
  1551.1 18.5 convolution_bitcast_fusion.3
  1581.5 20.1 fusion.99
  1607.4 22.2 fusion.134
  1629.6 28.1 add_convert_fusion.1.refs_2_
  1657.7 26.9 multiply_reduce_fusion.1
  1685.5 50.8 %multiply_convert_fusion = (bf16[4,4,384,1536]{3,2,1,0:T(8,128)(2,1)}, f32[4,4,384,1536]{3,2,1,0:T(8,128)}) fusion(f32[4,4,384]{2,1,0:T(4,128)S(1)} %copy-done.22, bf16[4,2048,1536]{2,1,0:T(8,128)(2,1)} %pad_maximum_fusion.1, s32[4,4,384]{2,1,0:T(4,128)S(1)} %slice.122), kind=kOutput, calls=%fused_computation.21 | convolution fusion | flops 38705037312 | bytes 81838080 | tf_op jit(solution)/shard_map/bect,btd->becd/dot_general | solution.py:172
  1736.3 49.3 %fusion.72 = bf16[4,4,384,1536]{3,2,1,0:T(8,128)(2,1)} fusion(bf16[4,2048,1536]{2,1,0:T(8,128)(2,1)} %pad_maximum_fusion, s32[4,4,384]{2,1,0:T(4,128)S(1)} %slice.122), kind=kOutput, calls=%fused_computation.87 | convolution fusion | flops 38676725760 | bytes 44064768 | tf_op jit(solution)/shard_map/bect,btd->becd/dot_general | solution.py:171
  1785.6 23.3 fusion.29
  1808.9 23.2 fusion.31
  1832.1 28.7 multiply_convert_fusion.4
  1860.8 20.2 fusion.102
  1899.4 18.5 convolution_bitcast_fusion.1
  1949.5 21.8 fusion.127
  1971.3 25.9 multiply_reduce_fusion
  1997.2 27.9 add_convert_fusion.refs_3_
  2026.5 63.2 %shard_map.172 = f32[2,2048,1536]{2,1,0:T(8,128)} custom-call(s32[64]{0:T(128)} %reshape.78.cnt_ref, s32[24576]{0:T(1024)} %reshape.79.tok_ref, f32[24576]{0:T(1024)} %reshape_squeeze.3.gate_ref, bf16[4,4,384,1536]{3,2,1,0:T(8,128)(2,1)} %add_convert_fusion.3.refs_0_, bf16[4,4,384,1536]{3,2,1,0:T(8,128)(2,1)} %add_convert_fusion.2.refs_1_, ...), custom_call_target="tpu_custom_call" | custom-call | flops 20000000000 | bytes 130000000 | tf_op jit(solution)/shard_map/pallas_call | solution.py:71
  2096.1 64.4 %shard_map.170 = f32[2,2048,1536]{2,1,0:T(8,128)} custom-call(s32[64]{0:T(128)} %reshape.78.cnt_ref, s32[24576]{0:T(1024)} %reshape.79.tok_ref, f32[24576]{0:T(1024)} %reshape_squeeze.3.gate_ref, bf16[4,4,384,1536]{3,2,1,0:T(8,128)(2,1)} %get-tuple-element.89.refs_0_, bf16[4,4,384,1536]{3,2,1,0:T(8,128)(2,1)} %get-tuple-element.90.refs_1_, ...), custom_call_target="tpu_custom_call" | custom-call | flops 20000000000 | bytes 130000000 | tf_op jit(solution)/shard_map/pallas_call | solution.py:71
  2174.6 62.7 %shard_map.171 = f32[2,2048,1536]{2,1,0:T(8,128)} custom-call(s32[64]{0:T(128)} %reshape.78.cnt_ref, s32[24576]{0:T(1024)} %reshape.79.tok_ref, f32[24576]{0:T(1024)} %reshape_squeeze.3.gate_ref, bf16[4,4,384,1536]{3,2,1,0:T(8,128)(2,1)} %add_convert_fusion.3.refs_0_, bf16[4,4,384,1536]{3,2,1,0:T(8,128)(2,1)} %add_convert_fusion.2.refs_1_, ...), custom_call_target="tpu_custom_call" | custom-call | flops 20000000000 | bytes 130000000 | tf_op jit(solution)/shard_map/pallas_call | solution.py:71
  2244.9 63.4 %collective-permute-done.28 = f32[4,768,512]{2,1,0:T(8,128)} collective-permute-done((f32[4,768,512]{2,1,0:T(8,128)}, f32[4,768,512]{2,1,0:T(8,128)}, u32[]{:S(2)}, u32[]{:S(2)}) %collective-permute-start.28) | collective-permute-done | bytes 6291488 | tf_op jit(solution)/shard_map/ppermute | solution.py:188
  2310.3 63.9 %shard_map.169 = f32[2,2048,1536]{2,1,0:T(8,128)} custom-call(s32[64]{0:T(128)} %reshape.78.cnt_ref, s32[24576]{0:T(1024)} %reshape.79.tok_ref, f32[24576]{0:T(1024)} %reshape_squeeze.3.gate_ref, bf16[4,4,384,1536]{3,2,1,0:T(8,128)(2,1)} %get-tuple-element.89.refs_0_, bf16[4,4,384,1536]{3,2,1,0:T(8,128)(2,1)} %get-tuple-element.90.refs_1_, ...), custom_call_target="tpu_custom_call" | custom-call | flops 20000000000 | bytes 130000000 | tf_op jit(solution)/shard_map/pallas_call | solution.py:71
  2389.4 53.6 %collective-permute-done.32 = f32[4,768,512]{2,1,0:T(8,128)} collective-permute-done((f32[4,768,512]{2,1,0:T(8,128)}, f32[4,768,512]{2,1,0:T(8,128)}, u32[]{:S(2)}, u32[]{:S(2)}) %collective-permute-start.32) | collective-permute-done | bytes 6291488 | tf_op jit(solution)/shard_map/ppermute | solution.py:188
  2455.9 121.9 %collective-permute-done.36 = f32[4,256,1536]{2,1,0:T(8,128)} collective-permute-done((f32[4,256,1536]{2,1,0:T(8,128)}, f32[4,256,1536]{2,1,0:T(8,128)}, u32[]{:S(2)}, u32[]{:S(2)}) %collective-permute-start.36) | collective-permute-done | bytes 6291488 | tf_op jit(solution)/shard_map/ppermute | solution.py:188
  2579.3 133.4 %collective-permute-done.29 = f32[4,768,512]{2,1,0:T(8,128)} collective-permute-done((f32[4,768,512]{2,1,0:T(8,128)}, f32[4,768,512]{2,1,0:T(8,128)}, u32[]{:S(2)}, u32[]{:S(2)}) %collective-permute-start.29) | collective-permute-done | bytes 6291488 | tf_op jit(solution)/shard_map/ppermute | solution.py:188
  2714.1 133.4 %collective-permute-done.33 = f32[4,768,512]{2,1,0:T(8,128)} collective-permute-done((f32[4,768,512]{2,1,0:T(8,128)}, f32[4,768,512]{2,1,0:T(8,128)}, u32[]{:S(2)}, u32[]{:S(2)}) %collective-permute-start.33) | collective-permute-done | bytes 6291488 | tf_op jit(solution)/shard_map/ppermute | solution.py:188
  2847.5 30.7 select_reduce_fusion
  2878.4 104.0 %collective-permute-done.37 = f32[4,256,1536]{2,1,0:T(8,128)} collective-permute-done((f32[4,256,1536]{2,1,0:T(8,128)}, f32[4,256,1536]{2,1,0:T(8,128)}, u32[]{:S(2)}, u32[]{:S(2)}) %collective-permute-start.37) | collective-permute-done | bytes 6291488 | tf_op jit(solution)/shard_map/ppermute | solution.py:188
  2988.2 28.9 reduce-scatter.13.cloned.1.call-done
  3130.9 124.3 %collective-permute-done.34 = f32[4,768,512]{2,1,0:T(8,128)} collective-permute-done((f32[4,768,512]{2,1,0:T(8,128)}, f32[4,768,512]{2,1,0:T(8,128)}, u32[]{:S(2)}, u32[]{:S(2)}) %collective-permute-start.34) | collective-permute-done | bytes 6291488 | tf_op jit(solution)/shard_map/ppermute | solution.py:188
  3265.4 124.6 %collective-permute-done.38 = f32[4,256,1536]{2,1,0:T(8,128)} collective-permute-done((f32[4,256,1536]{2,1,0:T(8,128)}, f32[4,256,1536]{2,1,0:T(8,128)}, u32[]{:S(2)}, u32[]{:S(2)}) %collective-permute-start.38) | collective-permute-done | bytes 6291488 | tf_op jit(solution)/shard_map/ppermute | solution.py:188
  3398.4 19.9 fusion.82
  3418.4 20.3 fusion.87
  3438.6 86.2 %collective-permute-done.35 = f32[4,768,512]{2,1,0:T(8,128)} collective-permute-done((f32[4,768,512]{2,1,0:T(8,128)}, f32[4,768,512]{2,1,0:T(8,128)}, u32[]{:S(2)}, u32[]{:S(2)}) %collective-permute-start.35) | collective-permute-done | bytes 6291488 | tf_op jit(solution)/shard_map/ppermute | solution.py:188
  3532.0 261.5 %collective-permute-done.39 = f32[4,256,1536]{2,1,0:T(8,128)} collective-permute-done((f32[4,256,1536]{2,1,0:T(8,128)}, f32[4,256,1536]{2,1,0:T(8,128)}, u32[]{:S(2)}, u32[]{:S(2)}) %collective-permute-start.39) | collective-permute-done | bytes 6291488 | tf_op jit(solution)/shard_map/ppermute | solution.py:188
  (280 shorter events, 588.9 us)
Async XLA Ops:
  7.2 167.5 %all-gather.9.cloned.1.call-start = ((), (), s32[]{:S(2)}) async-start(), calls=%async_computation.6 | async-start | bytes 3538944 | tf_op jit(solution)/shard_map/all_gather | solution.py:131
  7.9 178.4 %all-gather.5.cloned.1.call-start = ((), (), s32[]{:S(2)}) async-start(), calls=%async_computation.4 | async-start | bytes 3538944 | tf_op jit(solution)/shard_map/all_gather | solution.py:133
  8.7 189.9 %all-gather.7.cloned.1.call-start = ((), (), s32[]{:S(2)}) async-start(), calls=%async_computation.5 | async-start | bytes 3538944 | tf_op jit(solution)/shard_map/all_gather | solution.py:132
  9.4 1675.3 %reduce-scatter.7.cloned.1.call-start = ((), (), s32[]{:S(2)}) async-start(), calls=%async_computation.7 | async-start | bytes 7077888 | tf_op jit(solution)/shard_map/reduce_scatter | solution.py:163
  53.1 133.3 %copy-start.11 = (f32[64,2048]{1,0:T(8,128)}, f32[64,2048]{1,0:T(8,128)S(1)}, u32[]{:S(2)}) copy-start(f32[64,2048]{1,0:T(8,128)S(1)} %fusion.154) | copy-start | bytes 1572868
  167.4 5.7 collective-permute-start
  167.9 5.2 collective-permute-start.1
  173.1 1.4 collective-permute-start.2
  174.6 439.1 %copy-start.14 = (s32[4,16,384]{2,1,0:T(8,128)}, s32[4,16,384]{2,1,0:T(8,128)S(1)}, u32[]{:S(2)}) copy-start(s32[4,16,384]{2,1,0:T(8,128)S(1)} %get-tuple-element.88) | copy-start | bytes 294916
  288.5 1396.2 %reduce-scatter.9.cloned.1.call-start = ((), (), s32[]{:S(2)}) async-start(), calls=%async_computation.8 | async-start | bytes 7077888 | tf_op jit(solution)/shard_map/reduce_scatter | solution.py:163
  288.5 189.3 %collective-permute-start.8 = (bf16[2048,1536]{1,0:T(8,128)(2,1)}, bf16[2048,1536]{1,0:T(8,128)(2,1)}, u32[]{:S(2)}, u32[]{:S(2)}) collective-permute-start(bf16[2048,1536]{1,0:T(8,128)(2,1)} %param.11), channel_id=1, source_target_pairs={{0,2},{1,3},{2,0},{3,1},{4,6},{5,7},{6,4},{7,5}} | collective-permute-start | bytes 18874376 | tf_op jit(solution)/shard_map/ppermute | solution.py:98
  289.1 1395.6 %reduce-scatter.11.cloned.1.call-start = ((), (), s32[]{:S(2)}) async-start(), calls=%async_computation.9 | async-start | bytes 7077888 | tf_op jit(solution)/shard_map/reduce_scatter | solution.py:163
  289.1 322.6 %collective-permute-start.3 = (bf16[2048,1536]{1,0:T(8,128)(2,1)}, bf16[2048,1536]{1,0:T(8,128)(2,1)}, u32[]{:S(2)}, u32[]{:S(2)}) collective-permute-start(bf16[2048,1536]{1,0:T(8,128)(2,1)} %param.10), channel_id=1, source_target_pairs={{0,2},{1,3},{2,0},{3,1},{4,6},{5,7},{6,4},{7,5}} | collective-permute-start | bytes 18874376 | tf_op jit(solution)/shard_map/ppermute | solution.py:98
  290.6 323.2 %collective-permute-start.9 = (bf16[2048,1536]{1,0:T(8,128)(2,1)}, bf16[2048,1536]{1,0:T(8,128)(2,1)}, u32[]{:S(2)}, u32[]{:S(2)}) collective-permute-start(bf16[2048,1536]{1,0:T(8,128)(2,1)} %param.11), channel_id=1, source_target_pairs={{0,1},{1,0},{2,3},{3,2},{4,5},{5,4},{6,7},{7,6}} | collective-permute-start | bytes 18874376 | tf_op jit(solution)/shard_map/ppermute | solution.py:99
  477.8 137.4 %collective-permute-start.10 = (bf16[2048,1536]{1,0:T(8,128)(2,1)}, bf16[2048,1536]{1,0:T(8,128)(2,1)}, u32[]{:S(2)}, u32[]{:S(2)}) collective-permute-start(bf16[2048,1536]{1,0:T(8,128)(2,1)} %collective-permute-done.8), channel_id=1, source_target_pairs={{0,1},{1,0},{2,3},{3,2},{4,5},{5,4},{6,7},{7,6}} | collective-permute-start | bytes 18874376 | tf_op jit(solution)/shard_map/ppermute | solution.py:100
  477.8 160.6 %collective-permute-start.4 = (bf16[2048,1536]{1,0:T(8,128)(2,1)}, bf16[2048,1536]{1,0:T(8,128)(2,1)}, u32[]{:S(2)}, u32[]{:S(2)}) collective-permute-start(bf16[2048,1536]{1,0:T(8,128)(2,1)} %param.10), channel_id=1, source_target_pairs={{0,1},{1,0},{2,3},{3,2},{4,5},{5,4},{6,7},{7,6}} | collective-permute-start | bytes 18874376 | tf_op jit(solution)/shard_map/ppermute | solution.py:99
  611.8 28.3 collective-permute-start.5
  611.8 185.8 %collective-permute-start.6 = (bf16[4,768,512]{2,1,0:T(8,128)(2,1)}, bf16[4,768,512]{2,1,0:T(8,128)(2,1)}, u32[]{:S(2)}, u32[]{:S(2)}) collective-permute-start(bf16[4,768,512]{2,1,0:T(8,128)(2,1)} %get-tuple-element.69), channel_id=1, source_target_pairs={{0,4},{4,0},{1,5},{5,1},{2,6},{6,2},{3,7},{7,3}} | collective-permute-start | bytes 9437192 | tf_op jit(solution)/shard_map/ppermute | solution.py:117
  613.7 2403.3 %reduce-scatter.13.cloned.1.call-start = ((), (), s32[]{:S(2)}) async-start(), calls=%async_computation.10 | async-start | bytes 884736
  613.8 161.9 %collective-permute-start.7 = (bf16[4,768,512]{2,1,0:T(8,128)(2,1)}, bf16[4,768,512]{2,1,0:T(8,128)(2,1)}, u32[]{:S(2)}, u32[]{:S(2)}) collective-permute-start(bf16[4,768,512]{2,1,0:T(8,128)(2,1)} %get-tuple-element.70), channel_id=1, source_target_pairs={{0,4},{4,0},{1,5},{5,1},{2,6},{6,2},{3,7},{7,3}} | collective-permute-start | bytes 9437192 | tf_op jit(solution)/shard_map/ppermute | solution.py:117
  615.2 228.0 %collective-permute-start.11 = (bf16[4,256,1536]{2,1,0:T(8,128)(2,1)}, bf16[4,256,1536]{2,1,0:T(8,128)(2,1)}, u32[]{:S(2)}, u32[]{:S(2)}) collective-permute-start(bf16[4,256,1536]{2,1,0:T(8,128)(2,1)} %get-tuple-element.71), channel_id=1, source_target_pairs={{0,4},{4,0},{1,5},{5,1},{2,6},{6,2},{3,7},{7,3}} | collective-permute-start | bytes 9437192 | tf_op jit(solution)/shard_map/ppermute | solution.py:117
  638.4 511.9 %collective-permute-start.12 = (bf16[4,768,512]{2,1,0:T(8,128)(2,1)}, bf16[4,768,512]{2,1,0:T(8,128)(2,1)}, u32[]{:S(2)}, u32[]{:S(2)}) collective-permute-start(bf16[4,768,512]{2,1,0:T(8,128)(2,1)} %get-tuple-element.73), channel_id=1, source_target_pairs={{0,4},{4,0},{1,5},{5,1},{2,6},{6,2},{3,7},{7,3}} | collective-permute-start | bytes 9437192 | tf_op jit(solution)/shard_map/ppermute | solution.py:117
  640.1 485.6 %collective-permute-start.13 = (bf16[4,768,512]{2,1,0:T(8,128)(2,1)}, bf16[4,768,512]{2,1,0:T(8,128)(2,1)}, u32[]{:S(2)}, u32[]{:S(2)}) collective-permute-start(bf16[4,768,512]{2,1,0:T(8,128)(2,1)} %get-tuple-element.74), channel_id=1, source_target_pairs={{0,4},{4,0},{1,5},{5,1},{2,6},{6,2},{3,7},{7,3}} | collective-permute-start | bytes 9437192 | tf_op jit(solution)/shard_map/ppermute | solution.py:117
  775.8 398.0 %collective-permute-start.14 = (bf16[4,256,1536]{2,1,0:T(8,128)(2,1)}, bf16[4,256,1536]{2,1,0:T(8,128)(2,1)}, u32[]{:S(2)}, u32[]{:S(2)}) collective-permute-start(bf16[4,256,1536]{2,1,0:T(8,128)(2,1)} %get-tuple-element.75), channel_id=1, source_target_pairs={{0,4},{4,0},{1,5},{5,1},{2,6},{6,2},{3,7},{7,3}} | collective-permute-start | bytes 9437192 | tf_op jit(solution)/shard_map/ppermute | solution.py:117
  797.6 683.1 %collective-permute-start.15 = (bf16[4,768,512]{2,1,0:T(8,128)(2,1)}, bf16[4,768,512]{2,1,0:T(8,128)(2,1)}, u32[]{:S(2)}, u32[]{:S(2)}) collective-permute-start(bf16[4,768,512]{2,1,0:T(8,128)(2,1)} %get-tuple-element.77), channel_id=1, source_target_pairs={{0,4},{4,0},{1,5},{5,1},{2,6},{6,2},{3,7},{7,3}} | collective-permute-start | bytes 9437192 | tf_op jit(solution)/shard_map/ppermute | solution.py:117
  843.2 613.3 %collective-permute-start.16 = (bf16[4,768,512]{2,1,0:T(8,128)(2,1)}, bf16[4,768,512]{2,1,0:T(8,128)(2,1)}, u32[]{:S(2)}, u32[]{:S(2)}) collective-permute-start(bf16[4,768,512]{2,1,0:T(8,128)(2,1)} %get-tuple-element.78), channel_id=1, source_target_pairs={{0,4},{4,0},{1,5},{5,1},{2,6},{6,2},{3,7},{7,3}} | collective-permute-start | bytes 9437192 | tf_op jit(solution)/shard_map/ppermute | solution.py:117
  1125.7 378.2 %collective-permute-start.17 = (bf16[4,256,1536]{2,1,0:T(8,128)(2,1)}, bf16[4,256,1536]{2,1,0:T(8,128)(2,1)}, u32[]{:S(2)}, u32[]{:S(2)}) collective-permute-start(bf16[4,256,1536]{2,1,0:T(8,128)(2,1)} %get-tuple-element.79), channel_id=1, source_target_pairs={{0,4},{4,0},{1,5},{5,1},{2,6},{6,2},{3,7},{7,3}} | collective-permute-start | bytes 9437192 | tf_op jit(solution)/shard_map/ppermute | solution.py:117
  1150.3 658.6 %collective-permute-start.18 = (bf16[4,768,512]{2,1,0:T(8,128)(2,1)}, bf16[4,768,512]{2,1,0:T(8,128)(2,1)}, u32[]{:S(2)}, u32[]{:S(2)}) collective-permute-start(bf16[4,768,512]{2,1,0:T(8,128)(2,1)} %get-tuple-element.85), channel_id=1, source_target_pairs={{0,4},{4,0},{1,5},{5,1},{2,6},{6,2},{3,7},{7,3}} | collective-permute-start | bytes 9437192 | tf_op jit(solution)/shard_map/ppermute | solution.py:117
  1173.8 611.8 %collective-permute-start.19 = (bf16[4,768,512]{2,1,0:T(8,128)(2,1)}, bf16[4,768,512]{2,1,0:T(8,128)(2,1)}, u32[]{:S(2)}, u32[]{:S(2)}) collective-permute-start(bf16[4,768,512]{2,1,0:T(8,128)(2,1)} %get-tuple-element.86), channel_id=1, source_target_pairs={{0,4},{4,0},{1,5},{5,1},{2,6},{6,2},{3,7},{7,3}} | collective-permute-start | bytes 9437192 | tf_op jit(solution)/shard_map/ppermute | solution.py:117
  1456.5 375.6 %collective-permute-start.20 = (bf16[4,256,1536]{2,1,0:T(8,128)(2,1)}, bf16[4,256,1536]{2,1,0:T(8,128)(2,1)}, u32[]{:S(2)}, u32[]{:S(2)}) collective-permute-start(bf16[4,256,1536]{2,1,0:T(8,128)(2,1)} %get-tuple-element.87), channel_id=1, source_target_pairs={{0,4},{4,0},{1,5},{5,1},{2,6},{6,2},{3,7},{7,3}} | collective-permute-start | bytes 9437192 | tf_op jit(solution)/shard_map/ppermute | solution.py:117
  2089.7 219.9 %collective-permute-start.23 = (f32[2,2048,1536]{2,1,0:T(8,128)}, f32[2,2048,1536]{2,1,0:T(8,128)}, u32[]{:S(2)}, u32[]{:S(2)}) collective-permute-start(f32[2,2048,1536]{2,1,0:T(8,128)} %shard_map.172), channel_id=1, source_target_pairs={{0,1},{1,0},{2,3},{3,2},{4,5},{5,4},{6,7},{7,6}} | collective-permute-start | bytes 75497480 | tf_op jit(solution)/shard_map/ppermute | solution.py:104
  2160.5 283.9 %collective-permute-start.21 = (f32[2,2048,1536]{2,1,0:T(8,128)}, f32[2,2048,1536]{2,1,0:T(8,128)}, u32[]{:S(2)}, u32[]{:S(2)}) collective-permute-start(f32[2,2048,1536]{2,1,0:T(8,128)} %shard_map.170), channel_id=1, source_target_pairs={{0,1},{1,0},{2,3},{3,2},{4,5},{5,4},{6,7},{7,6}} | collective-permute-start | bytes 75497480 | tf_op jit(solution)/shard_map/ppermute | solution.py:104
  2169.5 138.7 %collective-permute-start.28 = (f32[4,768,512]{2,1,0:T(8,128)}, f32[4,768,512]{2,1,0:T(8,128)}, u32[]{:S(2)}, u32[]{:S(2)}) collective-permute-start(f32[4,768,512]{2,1,0:T(8,128)} %constant_dynamic-slice_fusion.13), channel_id=1, source_target_pairs={{0,4},{4,0},{1,5},{5,1},{2,6},{6,2},{3,7},{7,3}} | collective-permute-start | bytes 18874376 | tf_op jit(solution)/shard_map/ppermute | solution.py:188
  2171.0 3.4 collective-permute-start.27
  2171.1 272.0 %collective-permute-start.32 = (f32[4,768,512]{2,1,0:T(8,128)}, f32[4,768,512]{2,1,0:T(8,128)}, u32[]{:S(2)}, u32[]{:S(2)}) collective-permute-start(f32[4,768,512]{2,1,0:T(8,128)} %constant_dynamic-slice_fusion.12), channel_id=1, source_target_pairs={{0,4},{4,0},{1,5},{5,1},{2,6},{6,2},{3,7},{7,3}} | collective-permute-start | bytes 18874376 | tf_op jit(solution)/shard_map/ppermute | solution.py:188
  2174.5 62.8 %collective-permute-start.26 = (f32[16,384]{1,0:T(8,128)S(1)}, f32[16,384]{1,0:T(8,128)S(1)}, u32[]{:S(2)}, u32[]{:S(2)}) collective-permute-start(f32[16,384]{1,0:T(8,128)S(1)} %get-tuple-element.159), channel_id=1, source_target_pairs={{0,1},{1,0},{2,3},{3,2},{4,5},{5,4},{6,7},{7,6}} | collective-permute-start | bytes 73736 | tf_op jit(solution)/shard_map/ppermute | solution.py:207
  2237.3 7.0 collective-permute-start.25
  2244.2 333.7 %collective-permute-start.36 = (f32[4,256,1536]{2,1,0:T(8,128)}, f32[4,256,1536]{2,1,0:T(8,128)}, u32[]{:S(2)}, u32[]{:S(2)}) collective-permute-start(f32[4,256,1536]{2,1,0:T(8,128)} %constant_dynamic-slice_fusion.14), channel_id=1, source_target_pairs={{0,4},{4,0},{1,5},{5,1},{2,6},{6,2},{3,7},{7,3}} | collective-permute-start | bytes 18874376 | tf_op jit(solution)/shard_map/ppermute | solution.py:188
  2308.2 404.5 %collective-permute-start.29 = (f32[4,768,512]{2,1,0:T(8,128)}, f32[4,768,512]{2,1,0:T(8,128)}, u32[]{:S(2)}, u32[]{:S(2)}) collective-permute-start(f32[4,768,512]{2,1,0:T(8,128)} %constant_dynamic-slice_fusion.10), channel_id=1, source_target_pairs={{0,4},{4,0},{1,5},{5,1},{2,6},{6,2},{3,7},{7,3}} | collective-permute-start | bytes 18874376 | tf_op jit(solution)/shard_map/ppermute | solution.py:188
  2309.6 537.9 %collective-permute-start.33 = (f32[4,768,512]{2,1,0:T(8,128)}, f32[4,768,512]{2,1,0:T(8,128)}, u32[]{:S(2)}, u32[]{:S(2)}) collective-permute-start(f32[4,768,512]{2,1,0:T(8,128)} %constant_dynamic-slice_fusion.9), channel_id=1, source_target_pairs={{0,4},{4,0},{1,5},{5,1},{2,6},{6,2},{3,7},{7,3}} | collective-permute-start | bytes 18874376 | tf_op jit(solution)/shard_map/ppermute | solution.py:188
  2374.2 610.3 %slice-start.2 = ((s8[6291456]{0:T(1024)(128)(4,1)}), s8[4194304]{0:T(1024)(128)(4,1)S(1)}, s32[]{:S(2)}) async-start(s8[6291456]{0:T(1024)(128)(4,1)} %bitcast.292), calls=%async_computation.13 | async-start | bytes 8388608
  2389.4 488.8 %copy-start.2 = (f32[2048,64]{0,1:T(8,128)S(1)}, f32[2048,64]{0,1:T(8,128)}, u32[]{:S(2)}) copy-start(f32[2048,64]{0,1:T(8,128)} %copy-done.1) | copy-start | bytes 1572868
  2389.4 488.8 %copy-start.17 = (f32[2048]{0:T(1024)S(1)}, f32[2048]{0:T(1024)}, u32[]{:S(2)}) copy-start(f32[2048]{0:T(1024)} %copy-done.16) | copy-start | bytes 24580
  2389.4 488.8 %copy-start.19 = (f32[2048]{0:T(1024)S(1)}, f32[2048]{0:T(1024)}, u32[]{:S(2)}) copy-start(f32[2048]{0:T(1024)} %copy-done.18) | copy-start | bytes 24580
  2389.4 595.2 %slice-start.3 = ((s8[6291456]{0:T(1024)(128)(4,1)}), s8[2097152]{0:T(1024)(128)(4,1)S(1)}, s32[]{:S(2)}) async-start(s8[6291456]{0:T(1024)(128)(4,1)} %bitcast.292), calls=%async_computation.14 | async-start | bytes 4194304
  2443.1 539.3 %collective-permute-start.37 = (f32[4,256,1536]{2,1,0:T(8,128)}, f32[4,256,1536]{2,1,0:T(8,128)}, u32[]{:S(2)}, u32[]{:S(2)}) collective-permute-start(f32[4,256,1536]{2,1,0:T(8,128)} %constant_dynamic-slice_fusion.11), channel_id=1, source_target_pairs={{0,4},{4,0},{1,5},{5,1},{2,6},{6,2},{3,7},{7,3}} | collective-permute-start | bytes 18874376 | tf_op jit(solution)/shard_map/ppermute | solution.py:188
  2444.4 954.0 %collective-permute-start.24 = (f32[2048,1536]{1,0:T(8,128)}, f32[2048,1536]{1,0:T(8,128)}, u32[]{:S(2)}, u32[]{:S(2)}) collective-permute-start(f32[2048,1536]{1,0:T(8,128)} %fusion.77), channel_id=1, source_target_pairs={{0,2},{1,3},{2,0},{3,1},{4,6},{5,7},{6,4},{7,5}} | collective-permute-start | bytes 37748744 | tf_op jit(solution)/shard_map/ppermute | solution.py:105
  2577.9 542.5 %collective-permute-start.30 = (f32[4,768,512]{2,1,0:T(8,128)}, f32[4,768,512]{2,1,0:T(8,128)}, u32[]{:S(2)}, u32[]{:S(2)}) collective-permute-start(f32[4,768,512]{2,1,0:T(8,128)} %constant_dynamic-slice_fusion.7), channel_id=1, source_target_pairs={{0,4},{4,0},{1,5},{5,1},{2,6},{6,2},{3,7},{7,3}} | collective-permute-start | bytes 18874376 | tf_op jit(solution)/shard_map/ppermute | solution.py:188
  2712.7 542.5 %collective-permute-start.34 = (f32[4,768,512]{2,1,0:T(8,128)}, f32[4,768,512]{2,1,0:T(8,128)}, u32[]{:S(2)}, u32[]{:S(2)}) collective-permute-start(f32[4,768,512]{2,1,0:T(8,128)} %constant_dynamic-slice_fusion.6), channel_id=1, source_target_pairs={{0,4},{4,0},{1,5},{5,1},{2,6},{6,2},{3,7},{7,3}} | collective-permute-start | bytes 18874376 | tf_op jit(solution)/shard_map/ppermute | solution.py:188
  2847.5 570.9 %collective-permute-start.22 = (f32[2048,1536]{1,0:T(8,128)}, f32[2048,1536]{1,0:T(8,128)}, u32[]{:S(2)}, u32[]{:S(2)}) collective-permute-start(f32[2048,1536]{1,0:T(8,128)} %fusion.83), channel_id=1, source_target_pairs={{0,2},{1,3},{2,0},{3,1},{4,6},{5,7},{6,4},{7,5}} | collective-permute-start | bytes 37748744 | tf_op jit(solution)/shard_map/ppermute | solution.py:105
  2982.4 407.6 %collective-permute-start.38 = (f32[4,256,1536]{2,1,0:T(8,128)}, f32[4,256,1536]{2,1,0:T(8,128)}, u32[]{:S(2)}, u32[]{:S(2)}) collective-permute-start(f32[4,256,1536]{2,1,0:T(8,128)} %constant_dynamic-slice_fusion.8), channel_id=1, source_target_pairs={{0,4},{4,0},{1,5},{5,1},{2,6},{6,2},{3,7},{7,3}} | collective-permute-start | bytes 18874376 | tf_op jit(solution)/shard_map/ppermute | solution.py:188
  3120.3 404.5 %collective-permute-start.35 = (f32[4,768,512]{2,1,0:T(8,128)}, f32[4,768,512]{2,1,0:T(8,128)}, u32[]{:S(2)}, u32[]{:S(2)}) collective-permute-start(f32[4,768,512]{2,1,0:T(8,128)} %get-tuple-element.110), channel_id=1, source_target_pairs={{0,4},{4,0},{1,5},{5,1},{2,6},{6,2},{3,7},{7,3}} | collective-permute-start | bytes 18874376 | tf_op jit(solution)/shard_map/ppermute | solution.py:188
  3121.7 269.7 %slice-start.13 = ((s8[12582912]{0:T(1024)(128)(4,1)}), s8[4194304]{0:T(1024)(128)(4,1)S(1)}, s32[]{:S(2)}) async-start(s8[12582912]{0:T(1024)(128)(4,1)} %bitcast.302), calls=%async_computation.24 | async-start | bytes 8388608
  3121.7 269.7 %slice-start.14 = ((s8[12582912]{0:T(1024)(128)(4,1)}), s8[4194304]{0:T(1024)(128)(4,1)S(1)}, s32[]{:S(2)}) async-start(s8[12582912]{0:T(1024)(128)(4,1)} %bitcast.302), calls=%async_computation.25 | async-start | bytes 8388608
  3130.9 260.5 %slice-start.15 = ((s8[12582912]{0:T(1024)(128)(4,1)}), s8[4194304]{0:T(1024)(128)(4,1)S(1)}, s32[]{:S(2)}) async-start(s8[12582912]{0:T(1024)(128)(4,1)} %bitcast.302), calls=%async_computation.26 | async-start | bytes 8388608
  3255.2 545.2 %collective-permute-start.31 = (f32[4,768,512]{2,1,0:T(8,128)}, f32[4,768,512]{2,1,0:T(8,128)}, u32[]{:S(2)}, u32[]{:S(2)}) collective-permute-start(f32[4,768,512]{2,1,0:T(8,128)} %get-tuple-element.105), channel_id=1, source_target_pairs={{0,4},{4,0},{1,5},{5,1},{2,6},{6,2},{3,7},{7,3}} | collective-permute-start | bytes 18874376 | tf_op jit(solution)/shard_map/ppermute | solution.py:188
  3265.4 133.0 %copy-start.10 = (bf16[2048,64]{0,1:T(8,128)(2,1)S(1)}, bf16[2048,64]{0,1:T(8,128)(2,1)}, u32[]{:S(2)}) copy-start(bf16[2048,64]{0,1:T(8,128)(2,1)} %copy-done.9) | copy-start | bytes 786436
  3265.4 133.0 %copy-start.13 = (bf16[1536,64]{0,1:T(8,128)(2,1)S(1)}, bf16[1536,64]{0,1:T(8,128)(2,1)}, u32[]{:S(2)}) copy-start(bf16[1536,64]{0,1:T(8,128)(2,1)} %copy-done.12) | copy-start | bytes 589828
  3390.0 403.5 %collective-permute-start.39 = (f32[4,256,1536]{2,1,0:T(8,128)}, f32[4,256,1536]{2,1,0:T(8,128)}, u32[]{:S(2)}, u32[]{:S(2)}) collective-permute-start(f32[4,256,1536]{2,1,0:T(8,128)} %get-tuple-element.115), channel_id=1, source_target_pairs={{0,4},{4,0},{1,5},{5,1},{2,6},{6,2},{3,7},{7,3}} | collective-permute-start | bytes 18874376 | tf_op jit(solution)/shard_map/ppermute | solution.py:188
  3391.4 133.4 %slice-start.8 = ((s8[6291456]{0:T(1024)(128)(4,1)}), s8[4194304]{0:T(1024)(128)(4,1)S(1)}, s32[]{:S(2)}) async-start(s8[6291456]{0:T(1024)(128)(4,1)} %bitcast.298), calls=%async_computation.19 | async-start | bytes 8388608
  3438.6 354.9 %slice-start.6 = ((s8[6291456]{0:T(1024)(128)(4,1)}), s8[4194304]{0:T(1024)(128)(4,1)S(1)}, s32[]{:S(2)}) async-start(s8[6291456]{0:T(1024)(128)(4,1)} %bitcast.296), calls=%async_computation.17 | async-start | bytes 8388608
  3438.6 354.9 %slice-start.7 = ((s8[6291456]{0:T(1024)(128)(4,1)}), s8[2097152]{0:T(1024)(128)(4,1)S(1)}, s32[]{:S(2)}) async-start(s8[6291456]{0:T(1024)(128)(4,1)} %bitcast.296), calls=%async_computation.18 | async-start | bytes 4194304
  3524.8 275.6 %slice-start.4 = ((s8[6291456]{0:T(1024)(128)(4,1)}), s8[4194304]{0:T(1024)(128)(4,1)S(1)}, s32[]{:S(2)}) async-start(s8[6291456]{0:T(1024)(128)(4,1)} %bitcast.294), calls=%async_computation.15 | async-start | bytes 8388608
  3532.0 268.4 %slice-start.5 = ((s8[6291456]{0:T(1024)(128)(4,1)}), s8[2097152]{0:T(1024)(128)(4,1)S(1)}, s32[]{:S(2)}) async-start(s8[6291456]{0:T(1024)(128)(4,1)} %bitcast.294), calls=%async_computation.16 | async-start | bytes 4194304
  (35 other events, 913.8 us)
Sparse Core Ops, SparseCore 0:
  9.8 29.4 all-gather.8
  41.1 27.1 all-gather.4
  70.1 26.6 all-gather.6
  288.6 78.8 reduce-scatter.6
  371.2 78.8 reduce-scatter.8
  613.9 78.7 reduce-scatter.10
  2988.3 28.6 reduce-scatter.12

commit v2 on v1

--- a/solution.py
+++ b/solution.py
@@ -100,10 +100,6 @@
         both_val = lax.ppermute(chip_val, 'ep', swap_core)
         return lax.optimization_barrier(jnp.stack([val, chip_val, core_val, both_val]))
 
-    def collect(near, far):
-        recv = lax.ppermute(far, 'ep', swap_core)
-        return near[0] + recv[0] + lax.ppermute(near[1] + recv[1], 'ep', swap_chip)
-
     def local_step(x_loc, dy_loc, top_loc, wr_loc, wg_loc, wu_loc, wd_loc, sg_loc, su_loc, sd_loc):
         tok_count, top_k = top_loc.shape
         num_experts = wr_loc.shape[1]
@@ -122,12 +118,12 @@
             return lax.dynamic_slice_in_dim(full, (1 - dp_idx) * half, half, axis=1), lax.dynamic_slice_in_dim(full, dp_idx * half, half, axis=1)
 
         shards = [[w[ci * per_chunk:(ci + 1) * per_chunk] for w in (wd_loc, wg_loc, wu_loc)] for ci in range(CHUNKS)]
-        shards, x_loc, dy_loc, top_loc, wr_loc = lax.optimization_barrier((shards, x_loc, dy_loc, top_loc, wr_loc))
+        w_router = lax.all_gather(wr_loc, all_axes, axis=0, tiled=True)
+        shards, x_loc, dy_loc, top_loc, w_router = lax.optimization_barrier((shards, x_loc, dy_loc, top_loc, w_router))
         chunk_w = [[gather_dp(w) for w in shards[ci]] for ci in range(CHUNKS)]
 
         x_all = spread(x_loc)
         dy_all = spread(dy_loc)
-        w_router = lax.all_gather(wr_loc, all_axes, axis=0, tiled=True)
         s_gate = lax.all_gather(sg_loc, all_axes, axis=0, tiled=True)
         s_up = lax.all_gather(su_loc, all_axes, axis=0, tiled=True)
         s_down = lax.all_gather(sd_loc, all_axes, axis=0, tiled=True)
@@ -161,6 +157,17 @@
 
         toks, gs_gate, gs_up, gs_down, dx_shared, s_out = lax.optimization_barrier((toks, gs_gate, gs_up, gs_down, dx_shared, s_out))
         gs_gate, gs_up, gs_down = [lax.psum_scatter(g, all_axes, scatter_dimension=0, tiled=True) for g in (gs_gate, gs_up, gs_down)]
+        counts = jnp.sum((toks >= 0).astype(jnp.int32), axis=-1).reshape(-1)
+        safe_toks = jnp.maximum(toks, 0).reshape(-1)
+        flat_gates = gates.reshape(-1)
+        near_cnt = ep_size // 2
+
+        def collect(parts, weighted):
+            far = combine(parts, counts, safe_toks, flat_gates, tok_count, weighted, near_cnt, ep_size - near_cnt)
+            near = combine(parts, counts, safe_toks, flat_gates, tok_count, weighted, 0, near_cnt)
+            recv = lax.ppermute(far, 'ep', swap_core)
+            return near[0] + recv[0], near[1] + recv[1]
+
         out_parts, dx_parts, q_parts = [], [], []
         grads = []
         for ci in range(CHUNKS):
@@ -176,32 +183,27 @@
             hidden = (jax.nn.silu(gate_pre) * up_pre).astype(BF16)
             out_rows = jnp.einsum('ebcf,efd->ebcd', hidden, w_down, preferred_element_type=F32).astype(BF16)
             q_parts.append(jnp.einsum('becd,ebcd->bec', rows_dy, out_rows, preferred_element_type=F32))
+            out_parts.append(out_rows)
+            if ci == CHUNKS - 1:
+                y_near, y_pass = collect(out_parts, True)
+                rows_g, y_pass = lax.optimization_barrier((rows_g, y_pass))
+                y_across = lax.ppermute(y_pass, 'ep', swap_chip)
             d_hidden = jnp.einsum('becd,efd->ebcf', rows_g, w_down, preferred_element_type=F32)
             d_gate, d_up = silu_grads(d_hidden, gate_pre, up_pre)
             sent_down, kept_down = split_dp(jnp.einsum('ebcf,becd->efd', hidden, rows_g, preferred_element_type=F32))
             sent_gate, kept_gate = split_dp(jnp.einsum('becd,ebcf->edf', rows_x, d_gate, preferred_element_type=F32))
             sent_up, kept_up = split_dp(jnp.einsum('becd,ebcf->edf', rows_x, d_up, preferred_element_type=F32))
             dx_rows = (jnp.einsum('ebcf,edf->ebcd', d_gate, w_gate, preferred_element_type=F32) + jnp.einsum('ebcf,edf->ebcd', d_up, w_up, preferred_element_type=F32)).astype(BF16)
-            toks, sent_down, sent_gate, sent_up, out_rows, dx_rows = lax.optimization_barrier((toks, sent_down, sent_gate, sent_up, out_rows, dx_rows))
+            toks, sent_down, sent_gate, sent_up, dx_rows = lax.optimization_barrier((toks, sent_down, sent_gate, sent_up, dx_rows))
             if ci == CHUNKS - 2:
                 toks, gs_gate, gs_up, gs_down = lax.optimization_barrier((toks, gs_gate, gs_up, gs_down))
             recvs = [lax.ppermute(val, 'dp', swap_dp) for val in (sent_down, sent_gate, sent_up)]
             grads.append(([kept_down, kept_gate, kept_up], recvs))
-            out_parts.append(out_rows)
             dx_parts.append(dx_rows)
 
-        counts = jnp.sum((toks >= 0).astype(jnp.int32), axis=-1).reshape(-1)
-        safe_toks = jnp.maximum(toks, 0).reshape(-1)
-        flat_gates = gates.reshape(-1)
-        near_cnt = ep_size // 2
-
-        def join(parts, weighted):
-            far = combine(parts, counts, safe_toks, flat_gates, tok_count, weighted, near_cnt, ep_size - near_cnt)
-            near = combine(parts, counts, safe_toks, flat_gates, tok_count, weighted, 0, near_cnt)
-            return collect(near, far)
-
-        y_loc = (join(out_parts, True) + s_out).astype(BF16)
-        dx_routed = join(dx_parts, False)
+        dx_near, dx_pass = collect(dx_parts, False)
+        dx_routed = dx_near + lax.ppermute(dx_pass, 'ep', swap_chip)
+        y_loc = (y_near + y_across + s_out).astype(BF16)
 
         q_tab = jnp.concatenate(q_parts, axis=1)
         q_from = [q_tab[0], lax.ppermute(q_tab[1], 'ep', swap_chip), lax.ppermute(q_tab[2], 'ep', swap_core), lax.ppermute(q_tab[3], 'ep', swap_both)]

time: 3820 us -> 3910 us (1.024)
  waiting for transfers between devices: 1610 us -> 1680 us
    ppermute x12, waiting for transfers between devices: 1210 us -> 1250 us  [local_step(): lax.ppermute(val, 'dp', swap_dp)]
  transfers between devices with their start and end apart: 47 -> 47, of which waited for: 20 -> 21; matrix products, arithmetic and copies ran while one was open for 41% -> 40% of each run, Pallas kernels for 5% -> 3%
where the time goes in v2:
time: 3910 us; the launch traced here: 3900 us
  waiting for transfers between devices  1680 us (43%)
  matrix products  1370 us (35%)
  other arithmetic  325 us (8%)
  Pallas kernels  255 us (7%)
  local copies, waits for them, and re-layouts  171 us (4%)
  starting transfers between devices  55.6 us (1%)
    ppermute x12, waiting for transfers between devices, local_step(): lax.ppermute(val, 'dp', swap_dp)  1250 us
    ppermute x3, waiting for transfers between devices, spread(): chip_val = lax.ppermute(val, 'ep', swap_chip)  325 us
    pallas_call x4, Pallas kernels, combine(): pl.pallas_call(functools.partial(combine_kernel, num_parts, per_part, slo...  255 us
    dot_general x4, matrix products, local_step(): jnp.einsum('bect,btd->becd', pick, dy_all, preferred_element_type=F32)  203 us
    dot_general x4, matrix products, local_step(): jnp.einsum('bect,btd->becd', pick, x_all, preferred_element_type=F32)  198 us
    dot_general x4, matrix products, local_step(): jnp.einsum('becd,efd->ebcf', rows_g, w_down, preferred_element_type=F32)  114 us
    dot_general x4, matrix products, local_step(): jnp.einsum('ebcf,edf->ebcd', d_gate, w_gate, preferred_element_type=F32)  113 us
    dot_general x4, matrix products, local_step(): jnp.einsum('ebcf,efd->ebcd', hidden, w_down, preferred_element_type=F32)  108 us
  transfers between devices with their start and end apart: 47, of which 21 were waited for; matrix products, arithmetic and copies ran while one was open for 40% of the time, Pallas kernels for 3%

profile of v2, /device:TPU:0, one launch (start us, length us, event | category | flops | bytes accessed | tf_op | source)
XLA Modules:
  0.0 3895.7 jit_solution(7597612040843721374)
XLA Ops:
  36.0 18.8 fusion.188
  60.5 107.5 %select_reduce_fusion.2 = (f32[64,384]{1,0:T(8,128)S(1)}, f32[64,384]{1,0:T(8,128)S(1)}) fusion(f32[2048]{0:T(1024)S(1)} %add_convert_fusion.4, f32[64,2048]{1,0:T(8,128)S(1)} %fusion.154, f32[64,2048]{1,0:T(8,128)S(1)} %fusion.187), kind=kLoop, calls=%fused_computation.2 | loop fusion | flops 251609088 | bytes 1253376 | tf_op jit(solution)/shard_map/reduce_sum | solution.py:140
  291.5 187.0 %collective-permute-done.8 = bf16[2048,1536]{1,0:T(8,128)(2,1)} collective-permute-done((bf16[2048,1536]{1,0:T(8,128)(2,1)}, bf16[2048,1536]{1,0:T(8,128)(2,1)}, u32[]{:S(2)}, u32[]{:S(2)}) %collective-permute-start.8) | collective-permute-done | bytes 6291488 | tf_op jit(solution)/shard_map/ppermute | solution.py:98
  479.0 133.5 %collective-permute-done.3 = bf16[2048,1536]{1,0:T(8,128)(2,1)} collective-permute-done((bf16[2048,1536]{1,0:T(8,128)(2,1)}, bf16[2048,1536]{1,0:T(8,128)(2,1)}, u32[]{:S(2)}, u32[]{:S(2)}) %collective-permute-start.3) | collective-permute-done | bytes 6291488 | tf_op jit(solution)/shard_map/ppermute | solution.py:98
  617.4 22.7 pad_maximum_fusion.1
  660.5 50.6 %multiply_convert_fusion.3 = (bf16[4,4,384,1536]{3,2,1,0:T(8,128)(2,1)}, f32[4,4,384,1536]{3,2,1,0:T(8,128)}) fusion(f32[4,4,384]{2,1,0:T(4,128)S(1)} %get-tuple-element.159, bf16[4,2048,1536]{2,1,0:T(8,128)(2,1)} %pad_maximum_fusion.1, s32[4,4,384]{2,1,0:T(4,128)S(1)} %slice.115), kind=kOutput, calls=%fused_computation.27 | convolution fusion | flops 38705037312 | bytes 81838080 | tf_op jit(solution)/shard_map/bect,btd->becd/dot_general | solution.py:179
  711.1 49.7 %fusion.57 = bf16[4,4,384,1536]{3,2,1,0:T(8,128)(2,1)} fusion(bf16[4,2048,1536]{2,1,0:T(8,128)(2,1)} %pad_maximum_fusion, s32[4,4,384]{2,1,0:T(4,128)S(1)} %slice.115), kind=kOutput, calls=%fused_computation.84 | convolution fusion | flops 38676725760 | bytes 44064768 | tf_op jit(solution)/shard_map/bect,btd->becd/dot_general | solution.py:178
  776.6 21.2 fusion.53
  799.7 23.3 fusion.55
  823.0 20.9 collective-permute-done.11
  844.0 28.0 multiply_convert_fusion.13
  872.0 20.1 fusion.93
  947.6 21.9 fusion.148
  969.5 28.8 add_convert_fusion.3.refs_0_
  999.1 51.0 %multiply_convert_fusion.2 = (bf16[4,4,384,1536]{3,2,1,0:T(8,128)(2,1)}, f32[4,4,384,1536]{3,2,1,0:T(8,128)}) fusion(f32[4,4,384]{2,1,0:T(4,128)S(1)} %copy-done.24, bf16[4,2048,1536]{2,1,0:T(8,128)(2,1)} %pad_maximum_fusion.1, s32[4,4,384]{2,1,0:T(4,128)S(1)} %slice.118), kind=kOutput, calls=%fused_computation.25 | convolution fusion | flops 38705037312 | bytes 81838080 | tf_op jit(solution)/shard_map/bect,btd->becd/dot_general | solution.py:179
  1050.1 49.5 %fusion.62 = bf16[4,4,384,1536]{3,2,1,0:T(8,128)(2,1)} fusion(bf16[4,2048,1536]{2,1,0:T(8,128)(2,1)} %pad_maximum_fusion, s32[4,4,384]{2,1,0:T(4,128)S(1)} %slice.118), kind=kOutput, calls=%fused_computation.85 | convolution fusion | flops 38676725760 | bytes 44064768 | tf_op jit(solution)/shard_map/bect,btd->becd/dot_general | solution.py:178
  1101.5 23.6 fusion.45
  1125.2 22.9 fusion.47
  1150.1 28.5 multiply_convert_fusion.10
  1178.6 20.1 fusion.96
  1204.5 18.8 convolution_bitcast_fusion.4
  1253.6 22.1 fusion.141
  1275.7 28.0 add_convert_fusion.2.refs_1_
  1304.6 50.6 %multiply_convert_fusion.1 = (bf16[4,4,384,1536]{3,2,1,0:T(8,128)(2,1)}, f32[4,4,384,1536]{3,2,1,0:T(8,128)}) fusion(f32[4,4,384]{2,1,0:T(4,128)S(1)} %copy-done.23, bf16[4,2048,1536]{2,1,0:T(8,128)(2,1)} %pad_maximum_fusion.1, s32[4,4,384]{2,1,0:T(4,128)S(1)} %slice.120), kind=kOutput, calls=%fused_computation.23 | convolution fusion | flops 38705037312 | bytes 81838080 | tf_op jit(solution)/shard_map/bect,btd->becd/dot_general | solution.py:179
  1355.2 49.4 %fusion.67 = bf16[4,4,384,1536]{3,2,1,0:T(8,128)(2,1)} fusion(bf16[4,2048,1536]{2,1,0:T(8,128)(2,1)} %pad_maximum_fusion, s32[4,4,384]{2,1,0:T(4,128)S(1)} %slice.120), kind=kOutput, calls=%fused_computation.86 | convolution fusion | flops 38676725760 | bytes 44064768 | tf_op jit(solution)/shard_map/bect,btd->becd/dot_general | solution.py:178
  1404.7 23.3 fusion.37
  1428.0 21.1 fusion.39
  1449.1 28.6 multiply_convert_fusion.7
  1514.4 21.8 fusion.134
  1536.2 28.4 add_convert_fusion.1.refs_2_
  1564.6 20.1 fusion.99
  1600.7 27.6 multiply_reduce_fusion.3
  1628.2 26.6 multiply_reduce_fusion.2
  1654.9 26.7 multiply_reduce_fusion.1
  1682.4 50.8 %multiply_convert_fusion = (bf16[4,4,384,1536]{3,2,1,0:T(8,128)(2,1)}, f32[4,4,384,1536]{3,2,1,0:T(8,128)}) fusion(f32[4,4,384]{2,1,0:T(4,128)S(1)} %copy-done.22, bf16[4,2048,1536]{2,1,0:T(8,128)(2,1)} %pad_maximum_fusion.1, s32[4,4,384]{2,1,0:T(4,128)S(1)} %slice.122), kind=kOutput, calls=%fused_computation.21 | convolution fusion | flops 38705037312 | bytes 81838080 | tf_op jit(solution)/shard_map/bect,btd->becd/dot_general | solution.py:179
  1733.2 49.7 %fusion.72 = bf16[4,4,384,1536]{3,2,1,0:T(8,128)(2,1)} fusion(bf16[4,2048,1536]{2,1,0:T(8,128)(2,1)} %pad_maximum_fusion, s32[4,4,384]{2,1,0:T(4,128)S(1)} %slice.122), kind=kOutput, calls=%fused_computation.87 | convolution fusion | flops 38676725760 | bytes 44064768 | tf_op jit(solution)/shard_map/bect,btd->becd/dot_general | solution.py:178
  1782.9 23.0 fusion.31
  1805.9 25.9 multiply_convert_fusion.6
  1831.8 26.7 multiply_reduce_fusion
  1858.5 64.4 %shard_map.170 = f32[2,2048,1536]{2,1,0:T(8,128)} custom-call(s32[64]{0:T(128)} %reshape.78.cnt_ref, s32[24576]{0:T(1024)} %reshape.79.tok_ref, f32[24576]{0:T(1024)} %reshape_squeeze.3.gate_ref, bf16[4,4,384,1536]{3,2,1,0:T(8,128)(2,1)} %get-tuple-element.179.refs_0_, bf16[4,4,384,1536]{3,2,1,0:T(8,128)(2,1)} %get-tuple-element.177.refs_1_, ...), custom_call_target="tpu_custom_call" | custom-call | flops 20000000000 | bytes 130000000 | tf_op jit(solution)/shard_map/pallas_call | solution.py:71
  1930.0 64.3 %shard_map.169 = f32[2,2048,1536]{2,1,0:T(8,128)} custom-call(s32[64]{0:T(128)} %reshape.78.cnt_ref, s32[24576]{0:T(1024)} %reshape.79.tok_ref, f32[24576]{0:T(1024)} %reshape_squeeze.3.gate_ref, bf16[4,4,384,1536]{3,2,1,0:T(8,128)(2,1)} %get-tuple-element.179.refs_0_, bf16[4,4,384,1536]{3,2,1,0:T(8,128)(2,1)} %get-tuple-element.177.refs_1_, ...), custom_call_target="tpu_custom_call" | custom-call | flops 20000000000 | bytes 130000000 | tf_op jit(solution)/shard_map/pallas_call | solution.py:71
  2009.0 20.2 fusion.102
  2029.2 28.6 multiply_convert_fusion.4
  2076.3 18.8 convolution_bitcast_fusion.1
  2126.8 21.7 fusion.127
  2148.5 28.1 add_convert_fusion.refs_3_
  2176.7 63.3 %shard_map.172 = f32[2,2048,1536]{2,1,0:T(8,128)} custom-call(s32[64]{0:T(128)} %reshape.78.cnt_ref, s32[24576]{0:T(1024)} %reshape.79.tok_ref, f32[24576]{0:T(1024)} %reshape_squeeze.3.gate_ref, bf16[4,4,384,1536]{3,2,1,0:T(8,128)(2,1)} %add_convert_fusion.3.refs_0_, bf16[4,4,384,1536]{3,2,1,0:T(8,128)(2,1)} %add_convert_fusion.2.refs_1_, ...), custom_call_target="tpu_custom_call" | custom-call | flops 20000000000 | bytes 130000000 | tf_op jit(solution)/shard_map/pallas_call | solution.py:71
  2263.0 31.7 collective-permute-done.26
  2296.7 99.2 %collective-permute-done.28 = f32[4,768,512]{2,1,0:T(8,128)S(1)} collective-permute-done((f32[4,768,512]{2,1,0:T(8,128)S(1)}, f32[4,768,512]{2,1,0:T(8,128)S(1)}, u32[]{:S(2)}, u32[]{:S(2)}) %collective-permute-start.28) | collective-permute-done | bytes 6291488 | tf_op jit(solution)/shard_map/ppermute | solution.py:200
  2400.3 62.8 %shard_map.171 = f32[2,2048,1536]{2,1,0:T(8,128)} custom-call(s32[64]{0:T(128)} %reshape.78.cnt_ref, s32[24576]{0:T(1024)} %reshape.79.tok_ref, f32[24576]{0:T(1024)} %reshape_squeeze.3.gate_ref, bf16[4,4,384,1536]{3,2,1,0:T(8,128)(2,1)} %add_convert_fusion.3.refs_0_, bf16[4,4,384,1536]{3,2,1,0:T(8,128)(2,1)} %add_convert_fusion.2.refs_1_, ...), custom_call_target="tpu_custom_call" | custom-call | flops 20000000000 | bytes 130000000 | tf_op jit(solution)/shard_map/pallas_call | solution.py:71
  2463.1 67.7 %collective-permute-done.32 = f32[4,768,512]{2,1,0:T(8,128)} collective-permute-done((f32[4,768,512]{2,1,0:T(8,128)}, f32[4,768,512]{2,1,0:T(8,128)}, u32[]{:S(2)}, u32[]{:S(2)}) %collective-permute-start.32) | collective-permute-done | bytes 6291488 | tf_op jit(solution)/shard_map/ppermute | solution.py:200
  2546.9 118.7 %collective-permute-done.36 = f32[4,256,1536]{2,1,0:T(8,128)} collective-permute-done((f32[4,256,1536]{2,1,0:T(8,128)}, f32[4,256,1536]{2,1,0:T(8,128)}, u32[]{:S(2)}, u32[]{:S(2)}) %collective-permute-start.36) | collective-permute-done | bytes 6291488 | tf_op jit(solution)/shard_map/ppermute | solution.py:200
  2667.3 133.2 %collective-permute-done.29 = f32[4,768,512]{2,1,0:T(8,128)} collective-permute-done((f32[4,768,512]{2,1,0:T(8,128)}, f32[4,768,512]{2,1,0:T(8,128)}, u32[]{:S(2)}, u32[]{:S(2)}) %collective-permute-start.29) | collective-permute-done | bytes 6291488 | tf_op jit(solution)/shard_map/ppermute | solution.py:200
  2802.1 133.2 %collective-permute-done.33 = f32[4,768,512]{2,1,0:T(8,128)} collective-permute-done((f32[4,768,512]{2,1,0:T(8,128)}, f32[4,768,512]{2,1,0:T(8,128)}, u32[]{:S(2)}, u32[]{:S(2)}) %collective-permute-start.33) | collective-permute-done | bytes 6291488 | tf_op jit(solution)/shard_map/ppermute | solution.py:200
  2935.3 30.1 select_reduce_fusion
  2965.6 104.5 %collective-permute-done.37 = f32[4,256,1536]{2,1,0:T(8,128)S(1)} collective-permute-done((f32[4,256,1536]{2,1,0:T(8,128)}, f32[4,256,1536]{2,1,0:T(8,128)S(1)}, u32[]{:S(2)}, u32[]{:S(2)}) %collective-permute-start.37) | collective-permute-done | bytes 6291488 | tf_op jit(solution)/shard_map/ppermute | solution.py:200
  3076.1 29.8 reduce-scatter.13.cloned.1.call-done
  3218.9 124.1 %collective-permute-done.34 = f32[4,768,512]{2,1,0:T(8,128)} collective-permute-done((f32[4,768,512]{2,1,0:T(8,128)}, f32[4,768,512]{2,1,0:T(8,128)}, u32[]{:S(2)}, u32[]{:S(2)}) %collective-permute-start.34) | collective-permute-done | bytes 6291488 | tf_op jit(solution)/shard_map/ppermute | solution.py:200
  3353.4 124.4 %collective-permute-done.38 = f32[4,256,1536]{2,1,0:T(8,128)} collective-permute-done((f32[4,256,1536]{2,1,0:T(8,128)}, f32[4,256,1536]{2,1,0:T(8,128)}, u32[]{:S(2)}, u32[]{:S(2)}) %collective-permute-start.38) | collective-permute-done | bytes 6291488 | tf_op jit(solution)/shard_map/ppermute | solution.py:200
  3486.3 20.7 fusion.86
  3506.9 19.7 fusion.82
  3526.6 86.0 %collective-permute-done.35 = f32[4,768,512]{2,1,0:T(8,128)} collective-permute-done((f32[4,768,512]{2,1,0:T(8,128)}, f32[4,768,512]{2,1,0:T(8,128)}, u32[]{:S(2)}, u32[]{:S(2)}) %collective-permute-start.35) | collective-permute-done | bytes 6291488 | tf_op jit(solution)/shard_map/ppermute | solution.py:200
  3619.8 127.6 %collective-permute-done.39 = f32[4,256,1536]{2,1,0:T(8,128)} collective-permute-done((f32[4,256,1536]{2,1,0:T(8,128)}, f32[4,256,1536]{2,1,0:T(8,128)}, u32[]{:S(2)}, u32[]{:S(2)}) %collective-permute-start.39) | collective-permute-done | bytes 6291488 | tf_op jit(solution)/shard_map/ppermute | solution.py:200
  3754.3 127.0 %collective-permute-done.31 = f32[4,768,512]{2,1,0:T(8,128)} collective-permute-done((f32[4,768,512]{2,1,0:T(8,128)}, f32[4,768,512]{2,1,0:T(8,128)}, u32[]{:S(2)}, u32[]{:S(2)}) %collective-permute-start.31) | collective-permute-done | bytes 6291488 | tf_op jit(solution)/shard_map/ppermute | solution.py:200
  (297 shorter events, 631.8 us)
Async XLA Ops:
  7.2 168.2 %all-gather.9.cloned.1.call-start = ((), (), s32[]{:S(2)}) async-start(), calls=%async_computation.6 | async-start | bytes 3538944 | tf_op jit(solution)/shard_map/all_gather | solution.py:127
  7.9 179.2 %all-gather.5.cloned.1.call-start = ((), (), s32[]{:S(2)}) async-start(), calls=%async_computation.4 | async-start | bytes 3538944 | tf_op jit(solution)/shard_map/all_gather | solution.py:129
  8.7 190.7 %all-gather.7.cloned.1.call-start = ((), (), s32[]{:S(2)}) async-start(), calls=%async_computation.5 | async-start | bytes 3538944 | tf_op jit(solution)/shard_map/all_gather | solution.py:128
  9.4 1672.2 %reduce-scatter.7.cloned.1.call-start = ((), (), s32[]{:S(2)}) async-start(), calls=%async_computation.7 | async-start | bytes 7077888 | tf_op jit(solution)/shard_map/reduce_scatter | solution.py:159
  57.0 130.1 %copy-start.12 = (f32[64,2048]{1,0:T(8,128)}, f32[64,2048]{1,0:T(8,128)S(1)}, u32[]{:S(2)}) copy-start(f32[64,2048]{1,0:T(8,128)S(1)} %fusion.154) | copy-start | bytes 1572868
  168.1 5.7 collective-permute-start
  168.9 5.0 collective-permute-start.1
  173.8 1.4 collective-permute-start.2
  175.4 438.5 %copy-start.16 = (s32[4,16,384]{2,1,0:T(8,128)}, s32[4,16,384]{2,1,0:T(8,128)S(1)}, u32[]{:S(2)}) copy-start(s32[4,16,384]{2,1,0:T(8,128)S(1)} %get-tuple-element.81) | copy-start | bytes 294916
  289.2 1392.4 %reduce-scatter.9.cloned.1.call-start = ((), (), s32[]{:S(2)}) async-start(), calls=%async_computation.8 | async-start | bytes 7077888 | tf_op jit(solution)/shard_map/reduce_scatter | solution.py:159
  289.2 189.3 %collective-permute-start.8 = (bf16[2048,1536]{1,0:T(8,128)(2,1)}, bf16[2048,1536]{1,0:T(8,128)(2,1)}, u32[]{:S(2)}, u32[]{:S(2)}) collective-permute-start(bf16[2048,1536]{1,0:T(8,128)(2,1)} %param.11), channel_id=1, source_target_pairs={{0,2},{1,3},{2,0},{3,1},{4,6},{5,7},{6,4},{7,5}} | collective-permute-start | bytes 18874376 | tf_op jit(solution)/shard_map/ppermute | solution.py:98
  290.0 1391.6 %reduce-scatter.11.cloned.1.call-start = ((), (), s32[]{:S(2)}) async-start(), calls=%async_computation.9 | async-start | bytes 7077888 | tf_op jit(solution)/shard_map/reduce_scatter | solution.py:159
  290.2 322.3 %collective-permute-start.3 = (bf16[2048,1536]{1,0:T(8,128)(2,1)}, bf16[2048,1536]{1,0:T(8,128)(2,1)}, u32[]{:S(2)}, u32[]{:S(2)}) collective-permute-start(bf16[2048,1536]{1,0:T(8,128)(2,1)} %param.10), channel_id=1, source_target_pairs={{0,2},{1,3},{2,0},{3,1},{4,6},{5,7},{6,4},{7,5}} | collective-permute-start | bytes 18874376 | tf_op jit(solution)/shard_map/ppermute | solution.py:98
  291.5 323.8 %collective-permute-start.9 = (bf16[2048,1536]{1,0:T(8,128)(2,1)}, bf16[2048,1536]{1,0:T(8,128)(2,1)}, u32[]{:S(2)}, u32[]{:S(2)}) collective-permute-start(bf16[2048,1536]{1,0:T(8,128)(2,1)} %param.11), channel_id=1, source_target_pairs={{0,1},{1,0},{2,3},{3,2},{4,5},{5,4},{6,7},{7,6}} | collective-permute-start | bytes 18874376 | tf_op jit(solution)/shard_map/ppermute | solution.py:99
  478.5 138.8 %collective-permute-start.10 = (bf16[2048,1536]{1,0:T(8,128)(2,1)}, bf16[2048,1536]{1,0:T(8,128)(2,1)}, u32[]{:S(2)}, u32[]{:S(2)}) collective-permute-start(bf16[2048,1536]{1,0:T(8,128)(2,1)} %collective-permute-done.8), channel_id=1, source_target_pairs={{0,1},{1,0},{2,3},{3,2},{4,5},{5,4},{6,7},{7,6}} | collective-permute-start | bytes 18874376 | tf_op jit(solution)/shard_map/ppermute | solution.py:100
  478.5 161.6 %collective-permute-start.4 = (bf16[2048,1536]{1,0:T(8,128)(2,1)}, bf16[2048,1536]{1,0:T(8,128)(2,1)}, u32[]{:S(2)}, u32[]{:S(2)}) collective-permute-start(bf16[2048,1536]{1,0:T(8,128)(2,1)} %param.10), channel_id=1, source_target_pairs={{0,1},{1,0},{2,3},{3,2},{4,5},{5,4},{6,7},{7,6}} | collective-permute-start | bytes 18874376 | tf_op jit(solution)/shard_map/ppermute | solution.py:99
  612.5 29.4 collective-permute-start.5
  612.5 185.3 %collective-permute-start.6 = (bf16[4,768,512]{2,1,0:T(8,128)(2,1)}, bf16[4,768,512]{2,1,0:T(8,128)(2,1)}, u32[]{:S(2)}, u32[]{:S(2)}) collective-permute-start(bf16[4,768,512]{2,1,0:T(8,128)(2,1)} %get-tuple-element.66), channel_id=1, source_target_pairs={{0,4},{4,0},{1,5},{5,1},{2,6},{6,2},{3,7},{7,3}} | collective-permute-start | bytes 9437192 | tf_op jit(solution)/shard_map/ppermute | solution.py:113
  615.3 2490.6 %reduce-scatter.13.cloned.1.call-start = ((), (), s32[]{:S(2)}) async-start(), calls=%async_computation.10 | async-start | bytes 884736
  615.4 161.1 %collective-permute-start.7 = (bf16[4,768,512]{2,1,0:T(8,128)(2,1)}, bf16[4,768,512]{2,1,0:T(8,128)(2,1)}, u32[]{:S(2)}, u32[]{:S(2)}) collective-permute-start(bf16[4,768,512]{2,1,0:T(8,128)(2,1)} %get-tuple-element.67), channel_id=1, source_target_pairs={{0,4},{4,0},{1,5},{5,1},{2,6},{6,2},{3,7},{7,3}} | collective-permute-start | bytes 9437192 | tf_op jit(solution)/shard_map/ppermute | solution.py:113
  617.3 226.6 %collective-permute-start.11 = (bf16[4,256,1536]{2,1,0:T(8,128)(2,1)}, bf16[4,256,1536]{2,1,0:T(8,128)(2,1)}, u32[]{:S(2)}, u32[]{:S(2)}) collective-permute-start(bf16[4,256,1536]{2,1,0:T(8,128)(2,1)} %get-tuple-element.68), channel_id=1, source_target_pairs={{0,4},{4,0},{1,5},{5,1},{2,6},{6,2},{3,7},{7,3}} | collective-permute-start | bytes 9437192 | tf_op jit(solution)/shard_map/ppermute | solution.py:113
  640.1 485.0 %collective-permute-start.12 = (bf16[4,768,512]{2,1,0:T(8,128)(2,1)}, bf16[4,768,512]{2,1,0:T(8,128)(2,1)}, u32[]{:S(2)}, u32[]{:S(2)}) collective-permute-start(bf16[4,768,512]{2,1,0:T(8,128)(2,1)} %get-tuple-element.70), channel_id=1, source_target_pairs={{0,4},{4,0},{1,5},{5,1},{2,6},{6,2},{3,7},{7,3}} | collective-permute-start | bytes 9437192 | tf_op jit(solution)/shard_map/ppermute | solution.py:113
  641.9 457.7 %collective-permute-start.13 = (bf16[4,768,512]{2,1,0:T(8,128)(2,1)}, bf16[4,768,512]{2,1,0:T(8,128)(2,1)}, u32[]{:S(2)}, u32[]{:S(2)}) collective-permute-start(bf16[4,768,512]{2,1,0:T(8,128)(2,1)} %get-tuple-element.71), channel_id=1, source_target_pairs={{0,4},{4,0},{1,5},{5,1},{2,6},{6,2},{3,7},{7,3}} | collective-permute-start | bytes 9437192 | tf_op jit(solution)/shard_map/ppermute | solution.py:113
  776.5 371.6 %collective-permute-start.14 = (bf16[4,256,1536]{2,1,0:T(8,128)(2,1)}, bf16[4,256,1536]{2,1,0:T(8,128)(2,1)}, u32[]{:S(2)}, u32[]{:S(2)}) collective-permute-start(bf16[4,256,1536]{2,1,0:T(8,128)(2,1)} %get-tuple-element.72), channel_id=1, source_target_pairs={{0,4},{4,0},{1,5},{5,1},{2,6},{6,2},{3,7},{7,3}} | collective-permute-start | bytes 9437192 | tf_op jit(solution)/shard_map/ppermute | solution.py:113
  797.8 630.2 %collective-permute-start.15 = (bf16[4,768,512]{2,1,0:T(8,128)(2,1)}, bf16[4,768,512]{2,1,0:T(8,128)(2,1)}, u32[]{:S(2)}, u32[]{:S(2)}) collective-permute-start(bf16[4,768,512]{2,1,0:T(8,128)(2,1)} %get-tuple-element.74), channel_id=1, source_target_pairs={{0,4},{4,0},{1,5},{5,1},{2,6},{6,2},{3,7},{7,3}} | collective-permute-start | bytes 9437192 | tf_op jit(solution)/shard_map/ppermute | solution.py:113
  843.9 560.7 %collective-permute-start.16 = (bf16[4,768,512]{2,1,0:T(8,128)(2,1)}, bf16[4,768,512]{2,1,0:T(8,128)(2,1)}, u32[]{:S(2)}, u32[]{:S(2)}) collective-permute-start(bf16[4,768,512]{2,1,0:T(8,128)(2,1)} %get-tuple-element.75), channel_id=1, source_target_pairs={{0,4},{4,0},{1,5},{5,1},{2,6},{6,2},{3,7},{7,3}} | collective-permute-start | bytes 9437192 | tf_op jit(solution)/shard_map/ppermute | solution.py:113
  1099.6 349.4 %collective-permute-start.17 = (bf16[4,256,1536]{2,1,0:T(8,128)(2,1)}, bf16[4,256,1536]{2,1,0:T(8,128)(2,1)}, u32[]{:S(2)}, u32[]{:S(2)}) collective-permute-start(bf16[4,256,1536]{2,1,0:T(8,128)(2,1)} %get-tuple-element.76), channel_id=1, source_target_pairs={{0,4},{4,0},{1,5},{5,1},{2,6},{6,2},{3,7},{7,3}} | collective-permute-start | bytes 9437192 | tf_op jit(solution)/shard_map/ppermute | solution.py:113
  1125.1 657.8 %collective-permute-start.18 = (bf16[4,768,512]{2,1,0:T(8,128)(2,1)}, bf16[4,768,512]{2,1,0:T(8,128)(2,1)}, u32[]{:S(2)}, u32[]{:S(2)}) collective-permute-start(bf16[4,768,512]{2,1,0:T(8,128)(2,1)} %get-tuple-element.82), channel_id=1, source_target_pairs={{0,4},{4,0},{1,5},{5,1},{2,6},{6,2},{3,7},{7,3}} | collective-permute-start | bytes 9437192 | tf_op jit(solution)/shard_map/ppermute | solution.py:113
  1148.1 657.8 %collective-permute-start.19 = (bf16[4,768,512]{2,1,0:T(8,128)(2,1)}, bf16[4,768,512]{2,1,0:T(8,128)(2,1)}, u32[]{:S(2)}, u32[]{:S(2)}) collective-permute-start(bf16[4,768,512]{2,1,0:T(8,128)(2,1)} %get-tuple-element.83), channel_id=1, source_target_pairs={{0,4},{4,0},{1,5},{5,1},{2,6},{6,2},{3,7},{7,3}} | collective-permute-start | bytes 9437192 | tf_op jit(solution)/shard_map/ppermute | solution.py:113
  1404.6 427.3 %collective-permute-start.20 = (bf16[4,256,1536]{2,1,0:T(8,128)(2,1)}, bf16[4,256,1536]{2,1,0:T(8,128)(2,1)}, u32[]{:S(2)}, u32[]{:S(2)}) collective-permute-start(bf16[4,256,1536]{2,1,0:T(8,128)(2,1)} %get-tuple-element.84), channel_id=1, source_target_pairs={{0,4},{4,0},{1,5},{5,1},{2,6},{6,2},{3,7},{7,3}} | collective-permute-start | bytes 9437192 | tf_op jit(solution)/shard_map/ppermute | solution.py:113
  1923.0 71.4 %collective-permute-start.21 = (f32[2,2048,1536]{2,1,0:T(8,128)}, f32[2,2048,1536]{2,1,0:T(8,128)}, u32[]{:S(2)}, u32[]{:S(2)}) collective-permute-start(f32[2,2048,1536]{2,1,0:T(8,128)} %shard_map.170), channel_id=1, source_target_pairs={{0,1},{1,0},{2,3},{3,2},{4,5},{5,4},{6,7},{7,6}} | collective-permute-start | bytes 75497480 | tf_op jit(solution)/shard_map/ppermute | solution.py:168
  2148.5 109.0 %slice-start.21 = ((s8[6291456]{0:T(1024)(128)(4,1)}), s8[2097152]{0:T(1024)(128)(4,1)S(1)}, s32[]{:S(2)}) async-start(s8[6291456]{0:T(1024)(128)(4,1)} %bitcast.311), calls=%async_computation.32 | async-start | bytes 4194304
  2240.0 292.4 %collective-permute-start.23 = (f32[2,2048,1536]{2,1,0:T(8,128)}, f32[2,2048,1536]{2,1,0:T(8,128)}, u32[]{:S(2)}, u32[]{:S(2)}) collective-permute-start(f32[2,2048,1536]{2,1,0:T(8,128)} %shard_map.172), channel_id=1, source_target_pairs={{0,1},{1,0},{2,3},{3,2},{4,5},{5,4},{6,7},{7,6}} | collective-permute-start | bytes 75497480 | tf_op jit(solution)/shard_map/ppermute | solution.py:168
  2257.5 138.4 %collective-permute-start.28 = (f32[4,768,512]{2,1,0:T(8,128)S(1)}, f32[4,768,512]{2,1,0:T(8,128)S(1)}, u32[]{:S(2)}, u32[]{:S(2)}) collective-permute-start(f32[4,768,512]{2,1,0:T(8,128)S(1)} %bitcast.312), channel_id=1, source_target_pairs={{0,4},{4,0},{1,5},{5,1},{2,6},{6,2},{3,7},{7,3}} | collective-permute-start | bytes 18874376 | tf_op jit(solution)/shard_map/ppermute | solution.py:200
  2259.1 271.7 %collective-permute-start.32 = (f32[4,768,512]{2,1,0:T(8,128)}, f32[4,768,512]{2,1,0:T(8,128)}, u32[]{:S(2)}, u32[]{:S(2)}) collective-permute-start(f32[4,768,512]{2,1,0:T(8,128)} %constant_dynamic-slice_fusion.12), channel_id=1, source_target_pairs={{0,4},{4,0},{1,5},{5,1},{2,6},{6,2},{3,7},{7,3}} | collective-permute-start | bytes 18874376 | tf_op jit(solution)/shard_map/ppermute | solution.py:200
  2259.7 3.3 collective-permute-start.27
  2259.7 34.9 collective-permute-start.26
  2263.0 33.3 collective-permute-start.25
  2294.6 371.0 %collective-permute-start.36 = (f32[4,256,1536]{2,1,0:T(8,128)}, f32[4,256,1536]{2,1,0:T(8,128)}, u32[]{:S(2)}, u32[]{:S(2)}) collective-permute-start(f32[4,256,1536]{2,1,0:T(8,128)} %constant_dynamic-slice_fusion.14), channel_id=1, source_target_pairs={{0,4},{4,0},{1,5},{5,1},{2,6},{6,2},{3,7},{7,3}} | collective-permute-start | bytes 18874376 | tf_op jit(solution)/shard_map/ppermute | solution.py:200
  2296.2 504.3 %collective-permute-start.29 = (f32[4,768,512]{2,1,0:T(8,128)}, f32[4,768,512]{2,1,0:T(8,128)}, u32[]{:S(2)}, u32[]{:S(2)}) collective-permute-start(f32[4,768,512]{2,1,0:T(8,128)} %constant_dynamic-slice_fusion.10), channel_id=1, source_target_pairs={{0,4},{4,0},{1,5},{5,1},{2,6},{6,2},{3,7},{7,3}} | collective-permute-start | bytes 18874376 | tf_op jit(solution)/shard_map/ppermute | solution.py:200
  2398.6 536.7 %collective-permute-start.33 = (f32[4,768,512]{2,1,0:T(8,128)}, f32[4,768,512]{2,1,0:T(8,128)}, u32[]{:S(2)}, u32[]{:S(2)}) collective-permute-start(f32[4,768,512]{2,1,0:T(8,128)} %constant_dynamic-slice_fusion.9), channel_id=1, source_target_pairs={{0,4},{4,0},{1,5},{5,1},{2,6},{6,2},{3,7},{7,3}} | collective-permute-start | bytes 18874376 | tf_op jit(solution)/shard_map/ppermute | solution.py:200
  2400.3 672.4 %slice-start.4 = ((s8[6291456]{0:T(1024)(128)(4,1)}), s8[4194304]{0:T(1024)(128)(4,1)S(1)}, s32[]{:S(2)}) async-start(s8[6291456]{0:T(1024)(128)(4,1)} %bitcast.296), calls=%async_computation.15 | async-start | bytes 8388608
  2400.3 672.4 %slice-start.5 = ((s8[6291456]{0:T(1024)(128)(4,1)}), s8[2097152]{0:T(1024)(128)(4,1)S(1)}, s32[]{:S(2)}) async-start(s8[6291456]{0:T(1024)(128)(4,1)} %bitcast.296), calls=%async_computation.16 | async-start | bytes 4194304
  2463.1 472.2 %copy-start.13 = (f32[64,2048]{1,0:T(8,128)S(1)}, f32[64,2048]{1,0:T(8,128)}, u32[]{:S(2)}) copy-start(f32[64,2048]{1,0:T(8,128)} %copy-done.12) | copy-start | bytes 1572868
  2463.1 502.3 %copy-start.1 = (f32[2048,64]{0,1:T(8,128)S(1)}, f32[2048,64]{0,1:T(8,128)}, u32[]{:S(2)}) copy-start(f32[2048,64]{0,1:T(8,128)} %copy-done) | copy-start | bytes 1572868
  2463.1 502.3 %copy-start.18 = (f32[2048]{0:T(1024)S(1)}, f32[2048]{0:T(1024)}, u32[]{:S(2)}) copy-start(f32[2048]{0:T(1024)} %copy-done.17) | copy-start | bytes 24580
  2463.1 502.3 %copy-start.20 = (f32[2048]{0:T(1024)S(1)}, f32[2048]{0:T(1024)}, u32[]{:S(2)}) copy-start(f32[2048]{0:T(1024)} %copy-done.19) | copy-start | bytes 24580
  2530.8 539.2 %collective-permute-start.37 = (f32[4,256,1536]{2,1,0:T(8,128)}, f32[4,256,1536]{2,1,0:T(8,128)S(1)}, u32[]{:S(2)}, u32[]{:S(2)}) collective-permute-start(f32[4,256,1536]{2,1,0:T(8,128)} %constant_dynamic-slice_fusion.11), channel_id=1, source_target_pairs={{0,4},{4,0},{1,5},{5,1},{2,6},{6,2},{3,7},{7,3}} | collective-permute-start | bytes 18874376 | tf_op jit(solution)/shard_map/ppermute | solution.py:200
  2532.4 953.8 %collective-permute-start.22 = (f32[2048,1536]{1,0:T(8,128)}, f32[2048,1536]{1,0:T(8,128)}, u32[]{:S(2)}, u32[]{:S(2)}) collective-permute-start(f32[2048,1536]{1,0:T(8,128)} %fusion.87), channel_id=1, source_target_pairs={{0,2},{1,3},{2,0},{3,1},{4,6},{5,7},{6,4},{7,5}} | collective-permute-start | bytes 37748744 | tf_op jit(solution)/shard_map/ppermute | solution.py:190
  2665.7 542.5 %collective-permute-start.30 = (f32[4,768,512]{2,1,0:T(8,128)}, f32[4,768,512]{2,1,0:T(8,128)}, u32[]{:S(2)}, u32[]{:S(2)}) collective-permute-start(f32[4,768,512]{2,1,0:T(8,128)} %constant_dynamic-slice_fusion.7), channel_id=1, source_target_pairs={{0,4},{4,0},{1,5},{5,1},{2,6},{6,2},{3,7},{7,3}} | collective-permute-start | bytes 18874376 | tf_op jit(solution)/shard_map/ppermute | solution.py:200
  2800.5 542.5 %collective-permute-start.34 = (f32[4,768,512]{2,1,0:T(8,128)}, f32[4,768,512]{2,1,0:T(8,128)}, u32[]{:S(2)}, u32[]{:S(2)}) collective-permute-start(f32[4,768,512]{2,1,0:T(8,128)} %constant_dynamic-slice_fusion.6), channel_id=1, source_target_pairs={{0,4},{4,0},{1,5},{5,1},{2,6},{6,2},{3,7},{7,3}} | collective-permute-start | bytes 18874376 | tf_op jit(solution)/shard_map/ppermute | solution.py:200
  2935.3 571.6 %collective-permute-start.24 = (f32[2048,1536]{1,0:T(8,128)}, f32[2048,1536]{1,0:T(8,128)}, u32[]{:S(2)}, u32[]{:S(2)}) collective-permute-start(f32[2048,1536]{1,0:T(8,128)} %fusion.77), channel_id=1, source_target_pairs={{0,2},{1,3},{2,0},{3,1},{4,6},{5,7},{6,4},{7,5}} | collective-permute-start | bytes 37748744 | tf_op jit(solution)/shard_map/ppermute | solution.py:205
  3070.0 407.7 %collective-permute-start.38 = (f32[4,256,1536]{2,1,0:T(8,128)}, f32[4,256,1536]{2,1,0:T(8,128)}, u32[]{:S(2)}, u32[]{:S(2)}) collective-permute-start(f32[4,256,1536]{2,1,0:T(8,128)} %constant_dynamic-slice_fusion.8), channel_id=1, source_target_pairs={{0,4},{4,0},{1,5},{5,1},{2,6},{6,2},{3,7},{7,3}} | collective-permute-start | bytes 18874376 | tf_op jit(solution)/shard_map/ppermute | solution.py:200
  3208.1 404.5 %collective-permute-start.35 = (f32[4,768,512]{2,1,0:T(8,128)}, f32[4,768,512]{2,1,0:T(8,128)}, u32[]{:S(2)}, u32[]{:S(2)}) collective-permute-start(f32[4,768,512]{2,1,0:T(8,128)} %get-tuple-element.104), channel_id=1, source_target_pairs={{0,4},{4,0},{1,5},{5,1},{2,6},{6,2},{3,7},{7,3}} | collective-permute-start | bytes 18874376 | tf_op jit(solution)/shard_map/ppermute | solution.py:200
  3209.7 268.1 %slice-start.18 = ((s8[12582912]{0:T(1024)(128)(4,1)}), s8[4194304]{0:T(1024)(128)(4,1)S(1)}, s32[]{:S(2)}) async-start(s8[12582912]{0:T(1024)(128)(4,1)} %bitcast.308), calls=%async_computation.29 | async-start | bytes 8388608
  3209.7 268.1 %slice-start.19 = ((s8[12582912]{0:T(1024)(128)(4,1)}), s8[4194304]{0:T(1024)(128)(4,1)S(1)}, s32[]{:S(2)}) async-start(s8[12582912]{0:T(1024)(128)(4,1)} %bitcast.308), calls=%async_computation.30 | async-start | bytes 8388608
  3218.9 258.9 %slice-start.20 = ((s8[12582912]{0:T(1024)(128)(4,1)}), s8[4194304]{0:T(1024)(128)(4,1)S(1)}, s32[]{:S(2)}) async-start(s8[12582912]{0:T(1024)(128)(4,1)} %bitcast.308), calls=%async_computation.31 | async-start | bytes 8388608
  3351.8 395.6 %collective-permute-start.39 = (f32[4,256,1536]{2,1,0:T(8,128)}, f32[4,256,1536]{2,1,0:T(8,128)}, u32[]{:S(2)}, u32[]{:S(2)}) collective-permute-start(f32[4,256,1536]{2,1,0:T(8,128)} %get-tuple-element.109), channel_id=1, source_target_pairs={{0,4},{4,0},{1,5},{5,1},{2,6},{6,2},{3,7},{7,3}} | collective-permute-start | bytes 18874376 | tf_op jit(solution)/shard_map/ppermute | solution.py:200
  3484.7 396.6 %collective-permute-start.31 = (f32[4,768,512]{2,1,0:T(8,128)}, f32[4,768,512]{2,1,0:T(8,128)}, u32[]{:S(2)}, u32[]{:S(2)}) collective-permute-start(f32[4,768,512]{2,1,0:T(8,128)} %get-tuple-element.99), channel_id=1, source_target_pairs={{0,4},{4,0},{1,5},{5,1},{2,6},{6,2},{3,7},{7,3}} | collective-permute-start | bytes 18874376 | tf_op jit(solution)/shard_map/ppermute | solution.py:200
  3486.3 126.3 %slice-start.10 = ((s8[6291456]{0:T(1024)(128)(4,1)}), s8[4194304]{0:T(1024)(128)(4,1)S(1)}, s32[]{:S(2)}) async-start(s8[6291456]{0:T(1024)(128)(4,1)} %bitcast.302), calls=%async_computation.21 | async-start | bytes 8388608
  3526.6 220.8 %slice-start.8 = ((s8[6291456]{0:T(1024)(128)(4,1)}), s8[4194304]{0:T(1024)(128)(4,1)S(1)}, s32[]{:S(2)}) async-start(s8[6291456]{0:T(1024)(128)(4,1)} %bitcast.300), calls=%async_computation.19 | async-start | bytes 8388608
  3526.6 220.8 %slice-start.9 = ((s8[6291456]{0:T(1024)(128)(4,1)}), s8[2097152]{0:T(1024)(128)(4,1)S(1)}, s32[]{:S(2)}) async-start(s8[6291456]{0:T(1024)(128)(4,1)} %bitcast.300), calls=%async_computation.20 | async-start | bytes 4194304
  3612.6 268.7 %slice-start.6 = ((s8[6291456]{0:T(1024)(128)(4,1)}), s8[4194304]{0:T(1024)(128)(4,1)S(1)}, s32[]{:S(2)}) async-start(s8[6291456]{0:T(1024)(128)(4,1)} %bitcast.298), calls=%async_computation.17 | async-start | bytes 8388608
  3619.8 261.5 %slice-start.7 = ((s8[6291456]{0:T(1024)(128)(4,1)}), s8[2097152]{0:T(1024)(128)(4,1)S(1)}, s32[]{:S(2)}) async-start(s8[6291456]{0:T(1024)(128)(4,1)} %bitcast.298), calls=%async_computation.18 | async-start | bytes 4194304
  (42 other events, 1104.6 us)
Sparse Core Ops, SparseCore 0:
  9.8 30.6 all-gather.8
  42.3 26.6 all-gather.4
  70.8 26.6 all-gather.6
  289.3 78.6 reduce-scatter.6
  371.8 78.8 reduce-scatter.8
  615.4 79.4 reduce-scatter.10
  3076.2 29.6 reduce-scatter.12
